TPU v7x, 8 devices: a whole 2x2x1 slice. The times are simulated.
8 devices in a mesh: fsdp: 8 (over z, y, x, core).
Axes of the slice: x: 2, y: 2, z: 1, core: 2. Of those that a mesh axis runs over, the one named last changes fastest.
Arguments:
- x: bfloat16 [4, 32768, 768], P(None, 'fsdp')
- g: bfloat16 [4, 32768, 768], P(None, 'fsdp')
- w1: bfloat16 [2, 768, 3072], P(None, 'fsdp')
- w2: bfloat16 [2, 3072, 768], P(None, 'fsdp')
Outputs:
- output 1: bfloat16 [4, 32768, 768], P(None, 'fsdp')
- output 2: float32 [2, 768, 3072], P(None, 'fsdp')
- output 3: float32 [2, 3072, 768], P(None, 'fsdp')
All inputs are finite; a program needn't handle non-finite values.
Results may differ from a plain program's by a relative error of at most 0.011625.
Values are sent between devices in bfloat16 or wider.
A program may use at most 1 GiB of HBM per device.

v0:
```python
import jax
import jax.numpy as jnp
from jax import lax
from jax.sharding import PartitionSpec as P

AX = "fsdp"


def _gelu_bwd(a, e):
    return jax.vjp(jax.nn.gelu, a)[1](e)[0]


def solution(mesh):
    spec = P(None, AX, None)

    def body(x, g, w1, w2):
        layers = w1.shape[0]

        def micro(acc, xg):
            cur, gy = xg
            saved = []
            for l in range(layers):
                v1 = lax.all_gather(w1[l], AX, axis=0, tiled=True)
                v2 = lax.all_gather(w2[l], AX, axis=0, tiled=True)
                a = jnp.dot(cur, v1, preferred_element_type=jnp.float32).astype(jnp.bfloat16)
                h = jax.nn.gelu(a.astype(jnp.float32)).astype(jnp.bfloat16)
                saved.append((cur, a))
                cur = (cur.astype(jnp.float32) + jnp.dot(h, v2, preferred_element_type=jnp.float32)).astype(jnp.bfloat16)
            d1, d2 = [None] * layers, [None] * layers
            for l in reversed(range(layers)):
                xl, a = saved[l]
                v2 = lax.all_gather(w2[l], AX, axis=0, tiled=True)
                h = jax.nn.gelu(a.astype(jnp.float32)).astype(jnp.bfloat16)
                e = jnp.dot(gy, v2.T, preferred_element_type=jnp.float32)
                da = _gelu_bwd(a.astype(jnp.float32), e).astype(jnp.bfloat16)
                p2 = jnp.dot(h.T, gy, preferred_element_type=jnp.float32)
                p1 = jnp.dot(xl.T, da, preferred_element_type=jnp.float32)
                d2[l] = acc[1][l] + lax.psum_scatter(p2, AX, scatter_dimension=0, tiled=True)
                d1[l] = acc[0][l] + lax.psum_scatter(p1, AX, scatter_dimension=0, tiled=True)
                if l > 0:
                    v1 = lax.all_gather(w1[l], AX, axis=0, tiled=True)
                    gy = (gy.astype(jnp.float32) + jnp.dot(da, v1.T, preferred_element_type=jnp.float32)).astype(jnp.bfloat16)
            return (jnp.stack(d1), jnp.stack(d2)), cur

        zeros = (jnp.zeros(w1.shape, jnp.float32), jnp.zeros(w2.shape, jnp.float32))
        (d1, d2), y = lax.scan(micro, zeros, (x, g))
        return y, d1, d2

    return jax.shard_map(body, mesh=mesh, in_specs=(spec, spec, spec, spec),
                         out_specs=(spec, spec, spec), check_vma=False)
```

profile of v0, /device:TPU:0, one launch (start us, length us, event | category | flops | bytes accessed | tf_op | source)
XLA Modules:
  0.0 2181.3 jit_solution(14870102439763130478)
XLA Ops:
  10.4 2164.2 %while.17 = (s32[]{:T(128)}, f32[2,96,3072]{2,1,0:T(8,128)}, f32[2,384,768]{2,1,0:T(8,128)}, bf16[4,4096,768]{2,1,0:T(8,128)(2,1)}, bf16[4,4096,768]{2,1,0:T(8,1...) while((s32[]{:T(128)}, f32[2,96,3072]{2,1,0:T(8,128)}, ...), condition=%wide.region_5.6_spmd, body=%wide.region_0.5_spmd.sunk | while | flops 213688516608 | bytes 729022848 | solution.py:46
  16.6 32.2 %all-gather.17.cloned.1.call-done = bf16[1,768,3072]{2,1,0:T(8,128)(2,1)} async-done(((bf16[1,96,3072]{2,1,0:T(8,128)(2,1)}), bf16[1,768,3072]{2,1,0:T(8,128)(2,1)}) %all-gather.17.cloned.1.call-update) | async-done | bytes 4718608 | tf_op jit(solution)/shard_map/while/body/eval_jaxpr/all_gather | solution.py:23
  48.8 26.8 %convolution_convert_fusion.4 = bf16[4096,3072]{1,0:T(8,128)(2,1)} fusion(bf16[4,4096,768]{2,1,0:T(8,128)(2,1)} %get-tuple-element.242, s32[]{:T(128)S(6)} %copy.12, bf16[1,768,3072]{2,1,0:T(8,128)(2,1)} %all-gather.17.cloned.1.call-done), kind=kOutput, calls=%fused_computation.33.clone.1 | convolution fusion | flops 19339935744 | bytes 36175876 | tf_op jit(solution)/shard_map/while/body/eval_jaxpr/dot_general | solution.py:25
  75.7 7.9 all-gather.19.cloned.1.call-done
  83.6 37.4 %add_convert_fusion.5 = bf16[4096,768]{1,0:T(8,128)(2,1)} fusion(bf16[4,4096,768]{2,1,0:T(8,128)(2,1)} %get-tuple-element.242, s32[]{:T(128)S(6)} %copy.12, bf16[1,3072,768]{2,1,0:T(8,128)(2,1)} %all-gather.19.cloned.1.call-done, bf16[4096,3072]{1,0:T(8,128)(2,1)} %convolution_convert_fusion.4), kind=kOutput, calls=%fused_computation.36.clone.1 | convolution fusion | flops 19462619136 | bytes 42467332 | tf_op jit(solution)/shard_map/while/body/eval_jaxpr/dot_general | solution.py:28
  121.0 27.1 %convolution_convert_fusion.5 = bf16[4096,3072]{1,0:T(8,128)(2,1)} fusion(bf16[4096,768]{1,0:T(8,128)(2,1)} %add_convert_fusion.5, bf16[1,768,3072]{2,1,0:T(8,128)(2,1)} %all-gather.21.cloned.1.call-done), kind=kOutput, calls=%fused_computation.32.clone.1 | convolution fusion | flops 19339935744 | bytes 36175872 | tf_op jit(solution)/shard_map/while/body/eval_jaxpr/dot_general | solution.py:25
  153.0 57.7 %fusion.144 = bf16[4096,3072]{1,0:T(8,128)(2,1)} fusion(bf16[4096,3072]{1,0:T(8,128)(2,1)} %convolution_convert_fusion.5, bf16[4,4096,768]{2,1,0:T(8,128)(2,1)} %get-tuple-element.243, s32[]{:T(128)S(6)} %copy.12, bf16[1,3072,768]{2,1,0:T(8,128)(2,1)} %all-gather.23.cloned.1.call-done), kind=kOutput, calls=%fused_computation.14.clone.2 | convolution fusion | flops 19591593984 | bytes 61341700 | tf_op jit(solution)/shard_map/while/body/eval_jaxpr/dot_general | solution.py:34
  210.7 26.1 %add_convert_fusion.6 = bf16[4096,768]{1,0:T(8,128)(2,1)} fusion(bf16[4096,3072]{1,0:T(8,128)(2,1)} %fusion.144, bf16[4,4096,768]{2,1,0:T(8,128)(2,1)} %get-tuple-element.243, s32[]{:T(128)S(6)} %copy.12, bf16[1,768,3072]{2,1,0:T(8,128)(2,1)S(1)} %bitcast.129), kind=kOutput, calls=%fused_computation.35.clone.1 | convolution fusion | flops 19336790016 | bytes 42467332 | tf_op jit(solution)/shard_map/while/body/eval_jaxpr/dot_general | solution.py:42
  236.8 33.1 %fusion.149 = f32[3072,768]{1,0:T(8,128)} fusion(bf16[4096,768]{1,0:T(8,128)(2,1)} %add_convert_fusion.6, bf16[4096,3072]{1,0:T(8,128)(2,1)} %convolution_convert_fusion.4), kind=kOutput, calls=%fused_computation.74.clone.1 | convolution fusion | flops 19453181952 | bytes 40894464 | tf_op jit(solution)/shard_map/while/body/eval_jaxpr/dot_general | solution.py:36
  269.9 33.0 %fusion.150 = f32[3072,768]{1,0:T(8,128)} fusion(bf16[4,4096,768]{2,1,0:T(8,128)(2,1)} %get-tuple-element.243, s32[]{:T(128)S(6)} %copy.12, bf16[4096,3072]{1,0:T(8,128)(2,1)} %convolution_convert_fusion.5), kind=kOutput, calls=%fused_computation.38.clone.1 | convolution fusion | flops 19453181952 | bytes 40894468 | tf_op jit(solution)/shard_map/while/body/eval_jaxpr/dot_general | solution.py:36
  303.0 26.8 %fusion.147 = f32[768,3072]{1,0:T(8,128)} fusion(bf16[4096,768]{1,0:T(8,128)(2,1)} %add_convert_fusion.5, bf16[4096,3072]{1,0:T(8,128)(2,1)} %fusion.144), kind=kOutput, calls=%fused_computation.77.clone.1 | convolution fusion | flops 19327352832 | bytes 40894464 | tf_op jit(solution)/shard_map/while/body/eval_jaxpr/dot_general | solution.py:37
  329.9 57.5 %fusion.145 = bf16[4096,3072]{1,0:T(8,128)(2,1)} fusion(bf16[4096,3072]{1,0:T(8,128)(2,1)} %convolution_convert_fusion.4, bf16[4096,768]{1,0:T(8,128)(2,1)} %add_convert_fusion.6, bf16[1,3072,768]{2,1,0:T(8,128)(2,1)} %all-gather.19.cloned.1.call-done), kind=kOutput, calls=%fused_computation.17.clone.clone.2.clone.1 | convolution fusion | flops 19591593984 | bytes 61341696 | tf_op jit(solution)/shard_map/while/body/eval_jaxpr/dot_general | solution.py:34
  387.4 27.4 %fusion.146 = f32[768,3072]{1,0:T(8,128)} fusion(bf16[4,4096,768]{2,1,0:T(8,128)(2,1)} %get-tuple-element.242, s32[]{:T(128)S(6)} %copy.12, bf16[4096,3072]{1,0:T(8,128)(2,1)} %fusion.145), kind=kOutput, calls=%fused_computation.30.clone.3 | convolution fusion | flops 19327352832 | bytes 40894468 | tf_op jit(solution)/shard_map/while/body/eval_jaxpr/dot_general | solution.py:37
  414.9 36.9 %bitcast_dynamic-update-slice_fusion.2 = bf16[4,4096,768]{2,1,0:T(8,128)(2,1)} fusion(bf16[4,4096,768]{2,1,0:T(8,128)(2,1)} %get-tuple-element.232, s32[]{:T(128)S(6)} %copy.12, bf16[4096,768]{1,0:T(8,128)(2,1)} %add_convert_fusion.5, bf16[1,3072,768]{2,1,0:T(8,128)(2,1)} %all-gather.23.cloned.1.call-done, ...), kind=kOutput, calls=%fused_computation.37.clone.1 | convolution fusion | flops 19462619136 | bytes 42467332 | tf_op jit(solution)/shard_map/while/body/eval_jaxpr/dot_general | solution.py:28
  455.9 23.1 %reduce-scatter.7.cloned.1.call-done = f32[96,3072]{1,0:T(8,128)} async-done(((f32[768,3072]{1,0:T(8,128)}), f32[96,3072]{1,0:T(8,128)}) %reduce-scatter.7.cloned.1.call-update) | async-done | bytes 1179664 | tf_op jit(solution)/shard_map/while/body/eval_jaxpr/reduce_scatter | solution.py:39
  479.1 70.9 %reduce-scatter.5.cloned.1.call-done = f32[96,3072]{1,0:T(8,128)} async-done(((f32[768,3072]{1,0:T(8,128)}), f32[96,3072]{1,0:T(8,128)}) %reduce-scatter.5.cloned.1.call-update) | async-done | bytes 1179664 | tf_op jit(solution)/shard_map/while/body/eval_jaxpr/reduce_scatter | solution.py:39
  559.8 29.4 %all-gather.17.cloned.1.call-done = bf16[1,768,3072]{2,1,0:T(8,128)(2,1)} async-done(((bf16[1,96,3072]{2,1,0:T(8,128)(2,1)}), bf16[1,768,3072]{2,1,0:T(8,128)(2,1)}) %all-gather.17.cloned.1.call-update) | async-done | bytes 4718608 | tf_op jit(solution)/shard_map/while/body/eval_jaxpr/all_gather | solution.py:23
  589.1 26.8 %convolution_convert_fusion.4 = bf16[4096,3072]{1,0:T(8,128)(2,1)} fusion(bf16[4,4096,768]{2,1,0:T(8,128)(2,1)} %get-tuple-element.242, s32[]{:T(128)S(6)} %copy.12, bf16[1,768,3072]{2,1,0:T(8,128)(2,1)} %all-gather.17.cloned.1.call-done), kind=kOutput, calls=%fused_computation.33.clone.1 | convolution fusion | flops 19339935744 | bytes 36175876 | tf_op jit(solution)/shard_map/while/body/eval_jaxpr/dot_general | solution.py:25
  616.0 7.8 all-gather.19.cloned.1.call-done
  623.8 37.0 %add_convert_fusion.5 = bf16[4096,768]{1,0:T(8,128)(2,1)} fusion(bf16[4,4096,768]{2,1,0:T(8,128)(2,1)} %get-tuple-element.242, s32[]{:T(128)S(6)} %copy.12, bf16[1,3072,768]{2,1,0:T(8,128)(2,1)} %all-gather.19.cloned.1.call-done, bf16[4096,3072]{1,0:T(8,128)(2,1)} %convolution_convert_fusion.4), kind=kOutput, calls=%fused_computation.36.clone.1 | convolution fusion | flops 19462619136 | bytes 42467332 | tf_op jit(solution)/shard_map/while/body/eval_jaxpr/dot_general | solution.py:28
  660.7 27.1 %convolution_convert_fusion.5 = bf16[4096,3072]{1,0:T(8,128)(2,1)} fusion(bf16[4096,768]{1,0:T(8,128)(2,1)} %add_convert_fusion.5, bf16[1,768,3072]{2,1,0:T(8,128)(2,1)} %all-gather.21.cloned.1.call-done), kind=kOutput, calls=%fused_computation.32.clone.1 | convolution fusion | flops 19339935744 | bytes 36175872 | tf_op jit(solution)/shard_map/while/body/eval_jaxpr/dot_general | solution.py:25
  687.9 5.3 all-gather.23.cloned.1.call-done
  693.2 58.0 %fusion.144 = bf16[4096,3072]{1,0:T(8,128)(2,1)} fusion(bf16[4096,3072]{1,0:T(8,128)(2,1)} %convolution_convert_fusion.5, bf16[4,4096,768]{2,1,0:T(8,128)(2,1)} %get-tuple-element.243, s32[]{:T(128)S(6)} %copy.12, bf16[1,3072,768]{2,1,0:T(8,128)(2,1)} %all-gather.23.cloned.1.call-done), kind=kOutput, calls=%fused_computation.14.clone.2 | convolution fusion | flops 19591593984 | bytes 61341700 | tf_op jit(solution)/shard_map/while/body/eval_jaxpr/dot_general | solution.py:34
  751.2 25.9 %add_convert_fusion.6 = bf16[4096,768]{1,0:T(8,128)(2,1)} fusion(bf16[4096,3072]{1,0:T(8,128)(2,1)} %fusion.144, bf16[4,4096,768]{2,1,0:T(8,128)(2,1)} %get-tuple-element.243, s32[]{:T(128)S(6)} %copy.12, bf16[1,768,3072]{2,1,0:T(8,128)(2,1)S(1)} %bitcast.129), kind=kOutput, calls=%fused_computation.35.clone.1 | convolution fusion | flops 19336790016 | bytes 42467332 | tf_op jit(solution)/shard_map/while/body/eval_jaxpr/dot_general | solution.py:42
  777.1 33.1 %fusion.149 = f32[3072,768]{1,0:T(8,128)} fusion(bf16[4096,768]{1,0:T(8,128)(2,1)} %add_convert_fusion.6, bf16[4096,3072]{1,0:T(8,128)(2,1)} %convolution_convert_fusion.4), kind=kOutput, calls=%fused_computation.74.clone.1 | convolution fusion | flops 19453181952 | bytes 40894464 | tf_op jit(solution)/shard_map/while/body/eval_jaxpr/dot_general | solution.py:36
  810.2 33.4 %fusion.150 = f32[3072,768]{1,0:T(8,128)} fusion(bf16[4,4096,768]{2,1,0:T(8,128)(2,1)} %get-tuple-element.243, s32[]{:T(128)S(6)} %copy.12, bf16[4096,3072]{1,0:T(8,128)(2,1)} %convolution_convert_fusion.5), kind=kOutput, calls=%fused_computation.38.clone.1 | convolution fusion | flops 19453181952 | bytes 40894468 | tf_op jit(solution)/shard_map/while/body/eval_jaxpr/dot_general | solution.py:36
  843.7 26.8 %fusion.147 = f32[768,3072]{1,0:T(8,128)} fusion(bf16[4096,768]{1,0:T(8,128)(2,1)} %add_convert_fusion.5, bf16[4096,3072]{1,0:T(8,128)(2,1)} %fusion.144), kind=kOutput, calls=%fused_computation.77.clone.1 | convolution fusion | flops 19327352832 | bytes 40894464 | tf_op jit(solution)/shard_map/while/body/eval_jaxpr/dot_general | solution.py:37
  870.6 57.7 %fusion.145 = bf16[4096,3072]{1,0:T(8,128)(2,1)} fusion(bf16[4096,3072]{1,0:T(8,128)(2,1)} %convolution_convert_fusion.4, bf16[4096,768]{1,0:T(8,128)(2,1)} %add_convert_fusion.6, bf16[1,3072,768]{2,1,0:T(8,128)(2,1)} %all-gather.19.cloned.1.call-done), kind=kOutput, calls=%fused_computation.17.clone.clone.2.clone.1 | convolution fusion | flops 19591593984 | bytes 61341696 | tf_op jit(solution)/shard_map/while/body/eval_jaxpr/dot_general | solution.py:34
  928.3 27.3 %fusion.146 = f32[768,3072]{1,0:T(8,128)} fusion(bf16[4,4096,768]{2,1,0:T(8,128)(2,1)} %get-tuple-element.242, s32[]{:T(128)S(6)} %copy.12, bf16[4096,3072]{1,0:T(8,128)(2,1)} %fusion.145), kind=kOutput, calls=%fused_computation.30.clone.3 | convolution fusion | flops 19327352832 | bytes 40894468 | tf_op jit(solution)/shard_map/while/body/eval_jaxpr/dot_general | solution.py:37
  955.7 36.9 %bitcast_dynamic-update-slice_fusion.2 = bf16[4,4096,768]{2,1,0:T(8,128)(2,1)} fusion(bf16[4,4096,768]{2,1,0:T(8,128)(2,1)} %get-tuple-element.232, s32[]{:T(128)S(6)} %copy.12, bf16[4096,768]{1,0:T(8,128)(2,1)} %add_convert_fusion.5, bf16[1,3072,768]{2,1,0:T(8,128)(2,1)} %all-gather.23.cloned.1.call-done, ...), kind=kOutput, calls=%fused_computation.37.clone.1 | convolution fusion | flops 19462619136 | bytes 42467332 | tf_op jit(solution)/shard_map/while/body/eval_jaxpr/dot_general | solution.py:28
  996.7 22.5 %reduce-scatter.7.cloned.1.call-done = f32[96,3072]{1,0:T(8,128)} async-done(((f32[768,3072]{1,0:T(8,128)}), f32[96,3072]{1,0:T(8,128)}) %reduce-scatter.7.cloned.1.call-update) | async-done | bytes 1179664 | tf_op jit(solution)/shard_map/while/body/eval_jaxpr/reduce_scatter | solution.py:39
  1019.2 70.7 %reduce-scatter.5.cloned.1.call-done = f32[96,3072]{1,0:T(8,128)} async-done(((f32[768,3072]{1,0:T(8,128)}), f32[96,3072]{1,0:T(8,128)}) %reduce-scatter.5.cloned.1.call-update) | async-done | bytes 1179664 | tf_op jit(solution)/shard_map/while/body/eval_jaxpr/reduce_scatter | solution.py:39
  1099.8 29.3 %all-gather.17.cloned.1.call-done = bf16[1,768,3072]{2,1,0:T(8,128)(2,1)} async-done(((bf16[1,96,3072]{2,1,0:T(8,128)(2,1)}), bf16[1,768,3072]{2,1,0:T(8,128)(2,1)}) %all-gather.17.cloned.1.call-update) | async-done | bytes 4718608 | tf_op jit(solution)/shard_map/while/body/eval_jaxpr/all_gather | solution.py:23
  1129.1 26.9 %convolution_convert_fusion.4 = bf16[4096,3072]{1,0:T(8,128)(2,1)} fusion(bf16[4,4096,768]{2,1,0:T(8,128)(2,1)} %get-tuple-element.242, s32[]{:T(128)S(6)} %copy.12, bf16[1,768,3072]{2,1,0:T(8,128)(2,1)} %all-gather.17.cloned.1.call-done), kind=kOutput, calls=%fused_computation.33.clone.1 | convolution fusion | flops 19339935744 | bytes 36175876 | tf_op jit(solution)/shard_map/while/body/eval_jaxpr/dot_general | solution.py:25
  1156.0 7.8 all-gather.19.cloned.1.call-done
  1163.7 37.0 %add_convert_fusion.5 = bf16[4096,768]{1,0:T(8,128)(2,1)} fusion(bf16[4,4096,768]{2,1,0:T(8,128)(2,1)} %get-tuple-element.242, s32[]{:T(128)S(6)} %copy.12, bf16[1,3072,768]{2,1,0:T(8,128)(2,1)} %all-gather.19.cloned.1.call-done, bf16[4096,3072]{1,0:T(8,128)(2,1)} %convolution_convert_fusion.4), kind=kOutput, calls=%fused_computation.36.clone.1 | convolution fusion | flops 19462619136 | bytes 42467332 | tf_op jit(solution)/shard_map/while/body/eval_jaxpr/dot_general | solution.py:28
  1200.8 27.3 %convolution_convert_fusion.5 = bf16[4096,3072]{1,0:T(8,128)(2,1)} fusion(bf16[4096,768]{1,0:T(8,128)(2,1)} %add_convert_fusion.5, bf16[1,768,3072]{2,1,0:T(8,128)(2,1)} %all-gather.21.cloned.1.call-done), kind=kOutput, calls=%fused_computation.32.clone.1 | convolution fusion | flops 19339935744 | bytes 36175872 | tf_op jit(solution)/shard_map/while/body/eval_jaxpr/dot_general | solution.py:25
  1228.1 5.1 all-gather.23.cloned.1.call-done
  1233.2 57.6 %fusion.144 = bf16[4096,3072]{1,0:T(8,128)(2,1)} fusion(bf16[4096,3072]{1,0:T(8,128)(2,1)} %convolution_convert_fusion.5, bf16[4,4096,768]{2,1,0:T(8,128)(2,1)} %get-tuple-element.243, s32[]{:T(128)S(6)} %copy.12, bf16[1,3072,768]{2,1,0:T(8,128)(2,1)} %all-gather.23.cloned.1.call-done), kind=kOutput, calls=%fused_computation.14.clone.2 | convolution fusion | flops 19591593984 | bytes 61341700 | tf_op jit(solution)/shard_map/while/body/eval_jaxpr/dot_general | solution.py:34
  1290.8 25.9 %add_convert_fusion.6 = bf16[4096,768]{1,0:T(8,128)(2,1)} fusion(bf16[4096,3072]{1,0:T(8,128)(2,1)} %fusion.144, bf16[4,4096,768]{2,1,0:T(8,128)(2,1)} %get-tuple-element.243, s32[]{:T(128)S(6)} %copy.12, bf16[1,768,3072]{2,1,0:T(8,128)(2,1)S(1)} %bitcast.129), kind=kOutput, calls=%fused_computation.35.clone.1 | convolution fusion | flops 19336790016 | bytes 42467332 | tf_op jit(solution)/shard_map/while/body/eval_jaxpr/dot_general | solution.py:42
  1316.7 33.1 %fusion.149 = f32[3072,768]{1,0:T(8,128)} fusion(bf16[4096,768]{1,0:T(8,128)(2,1)} %add_convert_fusion.6, bf16[4096,3072]{1,0:T(8,128)(2,1)} %convolution_convert_fusion.4), kind=kOutput, calls=%fused_computation.74.clone.1 | convolution fusion | flops 19453181952 | bytes 40894464 | tf_op jit(solution)/shard_map/while/body/eval_jaxpr/dot_general | solution.py:36
  1349.8 33.3 %fusion.150 = f32[3072,768]{1,0:T(8,128)} fusion(bf16[4,4096,768]{2,1,0:T(8,128)(2,1)} %get-tuple-element.243, s32[]{:T(128)S(6)} %copy.12, bf16[4096,3072]{1,0:T(8,128)(2,1)} %convolution_convert_fusion.5), kind=kOutput, calls=%fused_computation.38.clone.1 | convolution fusion | flops 19453181952 | bytes 40894468 | tf_op jit(solution)/shard_map/while/body/eval_jaxpr/dot_general | solution.py:36
  1383.2 26.8 %fusion.147 = f32[768,3072]{1,0:T(8,128)} fusion(bf16[4096,768]{1,0:T(8,128)(2,1)} %add_convert_fusion.5, bf16[4096,3072]{1,0:T(8,128)(2,1)} %fusion.144), kind=kOutput, calls=%fused_computation.77.clone.1 | convolution fusion | flops 19327352832 | bytes 40894464 | tf_op jit(solution)/shard_map/while/body/eval_jaxpr/dot_general | solution.py:37
  1410.0 57.5 %fusion.145 = bf16[4096,3072]{1,0:T(8,128)(2,1)} fusion(bf16[4096,3072]{1,0:T(8,128)(2,1)} %convolution_convert_fusion.4, bf16[4096,768]{1,0:T(8,128)(2,1)} %add_convert_fusion.6, bf16[1,3072,768]{2,1,0:T(8,128)(2,1)} %all-gather.19.cloned.1.call-done), kind=kOutput, calls=%fused_computation.17.clone.clone.2.clone.1 | convolution fusion | flops 19591593984 | bytes 61341696 | tf_op jit(solution)/shard_map/while/body/eval_jaxpr/dot_general | solution.py:34
  1467.5 27.3 %fusion.146 = f32[768,3072]{1,0:T(8,128)} fusion(bf16[4,4096,768]{2,1,0:T(8,128)(2,1)} %get-tuple-element.242, s32[]{:T(128)S(6)} %copy.12, bf16[4096,3072]{1,0:T(8,128)(2,1)} %fusion.145), kind=kOutput, calls=%fused_computation.30.clone.3 | convolution fusion | flops 19327352832 | bytes 40894468 | tf_op jit(solution)/shard_map/while/body/eval_jaxpr/dot_general | solution.py:37
  1494.8 36.9 %bitcast_dynamic-update-slice_fusion.2 = bf16[4,4096,768]{2,1,0:T(8,128)(2,1)} fusion(bf16[4,4096,768]{2,1,0:T(8,128)(2,1)} %get-tuple-element.232, s32[]{:T(128)S(6)} %copy.12, bf16[4096,768]{1,0:T(8,128)(2,1)} %add_convert_fusion.5, bf16[1,3072,768]{2,1,0:T(8,128)(2,1)} %all-gather.23.cloned.1.call-done, ...), kind=kOutput, calls=%fused_computation.37.clone.1 | convolution fusion | flops 19462619136 | bytes 42467332 | tf_op jit(solution)/shard_map/while/body/eval_jaxpr/dot_general | solution.py:28
  1535.9 23.2 %reduce-scatter.7.cloned.1.call-done = f32[96,3072]{1,0:T(8,128)} async-done(((f32[768,3072]{1,0:T(8,128)}), f32[96,3072]{1,0:T(8,128)}) %reduce-scatter.7.cloned.1.call-update) | async-done | bytes 1179664 | tf_op jit(solution)/shard_map/while/body/eval_jaxpr/reduce_scatter | solution.py:39
  1559.1 70.7 %reduce-scatter.5.cloned.1.call-done = f32[96,3072]{1,0:T(8,128)} async-done(((f32[768,3072]{1,0:T(8,128)}), f32[96,3072]{1,0:T(8,128)}) %reduce-scatter.5.cloned.1.call-update) | async-done | bytes 1179664 | tf_op jit(solution)/shard_map/while/body/eval_jaxpr/reduce_scatter | solution.py:39
  1639.8 29.4 %all-gather.17.cloned.1.call-done = bf16[1,768,3072]{2,1,0:T(8,128)(2,1)} async-done(((bf16[1,96,3072]{2,1,0:T(8,128)(2,1)}), bf16[1,768,3072]{2,1,0:T(8,128)(2,1)}) %all-gather.17.cloned.1.call-update) | async-done | bytes 4718608 | tf_op jit(solution)/shard_map/while/body/eval_jaxpr/all_gather | solution.py:23
  1669.1 26.9 %convolution_convert_fusion.4 = bf16[4096,3072]{1,0:T(8,128)(2,1)} fusion(bf16[4,4096,768]{2,1,0:T(8,128)(2,1)} %get-tuple-element.242, s32[]{:T(128)S(6)} %copy.12, bf16[1,768,3072]{2,1,0:T(8,128)(2,1)} %all-gather.17.cloned.1.call-done), kind=kOutput, calls=%fused_computation.33.clone.1 | convolution fusion | flops 19339935744 | bytes 36175876 | tf_op jit(solution)/shard_map/while/body/eval_jaxpr/dot_general | solution.py:25
  1696.0 7.8 all-gather.19.cloned.1.call-done
  1703.8 37.2 %add_convert_fusion.5 = bf16[4096,768]{1,0:T(8,128)(2,1)} fusion(bf16[4,4096,768]{2,1,0:T(8,128)(2,1)} %get-tuple-element.242, s32[]{:T(128)S(6)} %copy.12, bf16[1,3072,768]{2,1,0:T(8,128)(2,1)} %all-gather.19.cloned.1.call-done, bf16[4096,3072]{1,0:T(8,128)(2,1)} %convolution_convert_fusion.4), kind=kOutput, calls=%fused_computation.36.clone.1 | convolution fusion | flops 19462619136 | bytes 42467332 | tf_op jit(solution)/shard_map/while/body/eval_jaxpr/dot_general | solution.py:28
  1741.0 27.1 %convolution_convert_fusion.5 = bf16[4096,3072]{1,0:T(8,128)(2,1)} fusion(bf16[4096,768]{1,0:T(8,128)(2,1)} %add_convert_fusion.5, bf16[1,768,3072]{2,1,0:T(8,128)(2,1)} %all-gather.21.cloned.1.call-done), kind=kOutput, calls=%fused_computation.32.clone.1 | convolution fusion | flops 19339935744 | bytes 36175872 | tf_op jit(solution)/shard_map/while/body/eval_jaxpr/dot_general | solution.py:25
  1768.0 5.1 all-gather.23.cloned.1.call-done
  1773.2 57.7 %fusion.144 = bf16[4096,3072]{1,0:T(8,128)(2,1)} fusion(bf16[4096,3072]{1,0:T(8,128)(2,1)} %convolution_convert_fusion.5, bf16[4,4096,768]{2,1,0:T(8,128)(2,1)} %get-tuple-element.243, s32[]{:T(128)S(6)} %copy.12, bf16[1,3072,768]{2,1,0:T(8,128)(2,1)} %all-gather.23.cloned.1.call-done), kind=kOutput, calls=%fused_computation.14.clone.2 | convolution fusion | flops 19591593984 | bytes 61341700 | tf_op jit(solution)/shard_map/while/body/eval_jaxpr/dot_general | solution.py:34
  1830.8 26.1 %add_convert_fusion.6 = bf16[4096,768]{1,0:T(8,128)(2,1)} fusion(bf16[4096,3072]{1,0:T(8,128)(2,1)} %fusion.144, bf16[4,4096,768]{2,1,0:T(8,128)(2,1)} %get-tuple-element.243, s32[]{:T(128)S(6)} %copy.12, bf16[1,768,3072]{2,1,0:T(8,128)(2,1)S(1)} %bitcast.129), kind=kOutput, calls=%fused_computation.35.clone.1 | convolution fusion | flops 19336790016 | bytes 42467332 | tf_op jit(solution)/shard_map/while/body/eval_jaxpr/dot_general | solution.py:42
  1857.0 33.1 %fusion.149 = f32[3072,768]{1,0:T(8,128)} fusion(bf16[4096,768]{1,0:T(8,128)(2,1)} %add_convert_fusion.6, bf16[4096,3072]{1,0:T(8,128)(2,1)} %convolution_convert_fusion.4), kind=kOutput, calls=%fused_computation.74.clone.1 | convolution fusion | flops 19453181952 | bytes 40894464 | tf_op jit(solution)/shard_map/while/body/eval_jaxpr/dot_general | solution.py:36
  1890.1 33.1 %fusion.150 = f32[3072,768]{1,0:T(8,128)} fusion(bf16[4,4096,768]{2,1,0:T(8,128)(2,1)} %get-tuple-element.243, s32[]{:T(128)S(6)} %copy.12, bf16[4096,3072]{1,0:T(8,128)(2,1)} %convolution_convert_fusion.5), kind=kOutput, calls=%fused_computation.38.clone.1 | convolution fusion | flops 19453181952 | bytes 40894468 | tf_op jit(solution)/shard_map/while/body/eval_jaxpr/dot_general | solution.py:36
  1923.2 26.8 %fusion.147 = f32[768,3072]{1,0:T(8,128)} fusion(bf16[4096,768]{1,0:T(8,128)(2,1)} %add_convert_fusion.5, bf16[4096,3072]{1,0:T(8,128)(2,1)} %fusion.144), kind=kOutput, calls=%fused_computation.77.clone.1 | convolution fusion | flops 19327352832 | bytes 40894464 | tf_op jit(solution)/shard_map/while/body/eval_jaxpr/dot_general | solution.py:37
  1950.1 57.5 %fusion.145 = bf16[4096,3072]{1,0:T(8,128)(2,1)} fusion(bf16[4096,3072]{1,0:T(8,128)(2,1)} %convolution_convert_fusion.4, bf16[4096,768]{1,0:T(8,128)(2,1)} %add_convert_fusion.6, bf16[1,3072,768]{2,1,0:T(8,128)(2,1)} %all-gather.19.cloned.1.call-done), kind=kOutput, calls=%fused_computation.17.clone.clone.2.clone.1 | convolution fusion | flops 19591593984 | bytes 61341696 | tf_op jit(solution)/shard_map/while/body/eval_jaxpr/dot_general | solution.py:34
  2007.6 27.4 %fusion.146 = f32[768,3072]{1,0:T(8,128)} fusion(bf16[4,4096,768]{2,1,0:T(8,128)(2,1)} %get-tuple-element.242, s32[]{:T(128)S(6)} %copy.12, bf16[4096,3072]{1,0:T(8,128)(2,1)} %fusion.145), kind=kOutput, calls=%fused_computation.30.clone.3 | convolution fusion | flops 19327352832 | bytes 40894468 | tf_op jit(solution)/shard_map/while/body/eval_jaxpr/dot_general | solution.py:37
  2035.1 36.9 %bitcast_dynamic-update-slice_fusion.2 = bf16[4,4096,768]{2,1,0:T(8,128)(2,1)} fusion(bf16[4,4096,768]{2,1,0:T(8,128)(2,1)} %get-tuple-element.232, s32[]{:T(128)S(6)} %copy.12, bf16[4096,768]{1,0:T(8,128)(2,1)} %add_convert_fusion.5, bf16[1,3072,768]{2,1,0:T(8,128)(2,1)} %all-gather.23.cloned.1.call-done, ...), kind=kOutput, calls=%fused_computation.37.clone.1 | convolution fusion | flops 19462619136 | bytes 42467332 | tf_op jit(solution)/shard_map/while/body/eval_jaxpr/dot_general | solution.py:28
  2076.1 23.1 %reduce-scatter.7.cloned.1.call-done = f32[96,3072]{1,0:T(8,128)} async-done(((f32[768,3072]{1,0:T(8,128)}), f32[96,3072]{1,0:T(8,128)}) %reduce-scatter.7.cloned.1.call-update) | async-done | bytes 1179664 | tf_op jit(solution)/shard_map/while/body/eval_jaxpr/reduce_scatter | solution.py:39
  2099.2 70.9 %reduce-scatter.5.cloned.1.call-done = f32[96,3072]{1,0:T(8,128)} async-done(((f32[768,3072]{1,0:T(8,128)}), f32[96,3072]{1,0:T(8,128)}) %reduce-scatter.5.cloned.1.call-update) | async-done | bytes 1179664 | tf_op jit(solution)/shard_map/while/body/eval_jaxpr/reduce_scatter | solution.py:39
  (132 shorter events, 64.2 us)
Async XLA Ops:
  10.4 38.4 %all-gather.17.cloned.1.call-start = ((), (), s32[]{:S(2)}) async-start(), calls=%async_computation.4 | async-start | bytes 5308416 | tf_op jit(solution)/shard_map/while/body/eval_jaxpr/all_gather | solution.py:23
  12.8 70.8 %all-gather.19.cloned.1.call-start = ((), (), s32[]{:S(2)}) async-start(), calls=%async_computation.5 | async-start | bytes 5308416 | tf_op jit(solution)/shard_map/while/body/eval_jaxpr/all_gather | solution.py:24
  15.2 105.8 %all-gather.21.cloned.1.call-start = ((), (), s32[]{:S(2)}) async-start(), calls=%async_computation.6 | async-start | bytes 5308416 | tf_op jit(solution)/shard_map/while/body/eval_jaxpr/all_gather | solution.py:23
  16.0 137.1 %all-gather.23.cloned.1.call-start = ((), (), s32[]{:S(2)}) async-start(), calls=%async_computation.7 | async-start | bytes 5308416 | tf_op jit(solution)/shard_map/while/body/eval_jaxpr/all_gather | solution.py:32
  16.5 435.2 %reduce-scatter.9.cloned.1.call-start = ((), (), s32[]{:S(2)}) async-start(), calls=%async_computation.10 | async-start | bytes 10616832 | tf_op jit(solution)/shard_map/while/body/eval_jaxpr/reduce_scatter | solution.py:38
  121.0 89.7 %slice-start = ((s8[4718592]{0:T(1024)(128)(4,1)}), s8[524288]{0:T(1024)(128)(4,1)S(1)}, s32[]{:S(2)}) async-start(s8[4718592]{0:T(1024)(128)(4,1)} %bitcast.128), calls=%async_computation.12 | async-start | bytes 1048576 | tf_op jit(solution)/shard_map/while
  153.0 57.7 %slice-start.1 = ((s8[4718592]{0:T(1024)(128)(4,1)}), s8[4194304]{0:T(1024)(128)(4,1)S(1)}, s32[]{:S(2)}) async-start(s8[4718592]{0:T(1024)(128)(4,1)} %bitcast.128), calls=%async_computation.13 | async-start | bytes 8388608 | tf_op jit(solution)/shard_map/while
  269.9 181.8 %reduce-scatter.11.cloned.1.call-start = ((), (), s32[]{:S(2)}) async-start(), calls=%async_computation.11 | async-start | bytes 10616832 | tf_op jit(solution)/shard_map/while/body/eval_jaxpr/reduce_scatter | solution.py:38
  303.0 176.1 %reduce-scatter.7.cloned.1.call-start = ((), (), s32[]{:S(2)}) async-start(), calls=%async_computation.9 | async-start | bytes 10616832 | tf_op jit(solution)/shard_map/while/body/eval_jaxpr/reduce_scatter | solution.py:39
  329.8 220.1 %reduce-scatter.5.cloned.1.call-start = ((), (), s32[]{:S(2)}) async-start(), calls=%async_computation.8 | async-start | bytes 10616832 | tf_op jit(solution)/shard_map/while/body/eval_jaxpr/reduce_scatter | solution.py:39
  414.8 135.1 %copy-start = (f32[2,96,3072]{2,1,0:T(8,128)S(1)}, f32[2,96,3072]{2,1,0:T(8,128)}, u32[]{:S(2)}) copy-start(f32[2,96,3072]{2,1,0:T(8,128)} %get-tuple-element.230) | copy-start | bytes 7077892 | tf_op jit(solution)/shard_map/while
  553.5 35.6 %all-gather.17.cloned.1.call-start = ((), (), s32[]{:S(2)}) async-start(), calls=%async_computation.4 | async-start | bytes 5308416 | tf_op jit(solution)/shard_map/while/body/eval_jaxpr/all_gather | solution.py:23
  556.0 67.8 %all-gather.19.cloned.1.call-start = ((), (), s32[]{:S(2)}) async-start(), calls=%async_computation.5 | async-start | bytes 5308416 | tf_op jit(solution)/shard_map/while/body/eval_jaxpr/all_gather | solution.py:24
  558.4 102.3 %all-gather.21.cloned.1.call-start = ((), (), s32[]{:S(2)}) async-start(), calls=%async_computation.6 | async-start | bytes 5308416 | tf_op jit(solution)/shard_map/while/body/eval_jaxpr/all_gather | solution.py:23
  559.2 134.0 %all-gather.23.cloned.1.call-start = ((), (), s32[]{:S(2)}) async-start(), calls=%async_computation.7 | async-start | bytes 5308416 | tf_op jit(solution)/shard_map/while/body/eval_jaxpr/all_gather | solution.py:32
  559.7 432.8 %reduce-scatter.9.cloned.1.call-start = ((), (), s32[]{:S(2)}) async-start(), calls=%async_computation.10 | async-start | bytes 10616832 | tf_op jit(solution)/shard_map/while/body/eval_jaxpr/reduce_scatter | solution.py:38
  660.7 90.5 %slice-start = ((s8[4718592]{0:T(1024)(128)(4,1)}), s8[524288]{0:T(1024)(128)(4,1)S(1)}, s32[]{:S(2)}) async-start(s8[4718592]{0:T(1024)(128)(4,1)} %bitcast.128), calls=%async_computation.12 | async-start | bytes 1048576 | tf_op jit(solution)/shard_map/while
  693.2 58.0 %slice-start.1 = ((s8[4718592]{0:T(1024)(128)(4,1)}), s8[4194304]{0:T(1024)(128)(4,1)S(1)}, s32[]{:S(2)}) async-start(s8[4718592]{0:T(1024)(128)(4,1)} %bitcast.128), calls=%async_computation.13 | async-start | bytes 8388608 | tf_op jit(solution)/shard_map/while
  810.2 182.4 %reduce-scatter.11.cloned.1.call-start = ((), (), s32[]{:S(2)}) async-start(), calls=%async_computation.11 | async-start | bytes 10616832 | tf_op jit(solution)/shard_map/while/body/eval_jaxpr/reduce_scatter | solution.py:38
  843.6 175.5 %reduce-scatter.7.cloned.1.call-start = ((), (), s32[]{:S(2)}) async-start(), calls=%async_computation.9 | async-start | bytes 10616832 | tf_op jit(solution)/shard_map/while/body/eval_jaxpr/reduce_scatter | solution.py:39
  870.5 219.4 %reduce-scatter.5.cloned.1.call-start = ((), (), s32[]{:S(2)}) async-start(), calls=%async_computation.8 | async-start | bytes 10616832 | tf_op jit(solution)/shard_map/while/body/eval_jaxpr/reduce_scatter | solution.py:39
  955.6 134.3 %copy-start = (f32[2,96,3072]{2,1,0:T(8,128)S(1)}, f32[2,96,3072]{2,1,0:T(8,128)}, u32[]{:S(2)}) copy-start(f32[2,96,3072]{2,1,0:T(8,128)} %get-tuple-element.230) | copy-start | bytes 7077892 | tf_op jit(solution)/shard_map/while
  1093.5 35.6 %all-gather.17.cloned.1.call-start = ((), (), s32[]{:S(2)}) async-start(), calls=%async_computation.4 | async-start | bytes 5308416 | tf_op jit(solution)/shard_map/while/body/eval_jaxpr/all_gather | solution.py:23
  1096.0 67.8 %all-gather.19.cloned.1.call-start = ((), (), s32[]{:S(2)}) async-start(), calls=%async_computation.5 | async-start | bytes 5308416 | tf_op jit(solution)/shard_map/while/body/eval_jaxpr/all_gather | solution.py:24
  1098.4 102.3 %all-gather.21.cloned.1.call-start = ((), (), s32[]{:S(2)}) async-start(), calls=%async_computation.6 | async-start | bytes 5308416 | tf_op jit(solution)/shard_map/while/body/eval_jaxpr/all_gather | solution.py:23
  1099.2 134.0 %all-gather.23.cloned.1.call-start = ((), (), s32[]{:S(2)}) async-start(), calls=%async_computation.7 | async-start | bytes 5308416 | tf_op jit(solution)/shard_map/while/body/eval_jaxpr/all_gather | solution.py:32
  1099.8 431.9 %reduce-scatter.9.cloned.1.call-start = ((), (), s32[]{:S(2)}) async-start(), calls=%async_computation.10 | async-start | bytes 10616832 | tf_op jit(solution)/shard_map/while/body/eval_jaxpr/reduce_scatter | solution.py:38
  1200.8 90.0 %slice-start = ((s8[4718592]{0:T(1024)(128)(4,1)}), s8[524288]{0:T(1024)(128)(4,1)S(1)}, s32[]{:S(2)}) async-start(s8[4718592]{0:T(1024)(128)(4,1)} %bitcast.128), calls=%async_computation.12 | async-start | bytes 1048576 | tf_op jit(solution)/shard_map/while
  1233.2 57.6 %slice-start.1 = ((s8[4718592]{0:T(1024)(128)(4,1)}), s8[4194304]{0:T(1024)(128)(4,1)S(1)}, s32[]{:S(2)}) async-start(s8[4718592]{0:T(1024)(128)(4,1)} %bitcast.128), calls=%async_computation.13 | async-start | bytes 8388608 | tf_op jit(solution)/shard_map/while
  1349.8 181.9 %reduce-scatter.11.cloned.1.call-start = ((), (), s32[]{:S(2)}) async-start(), calls=%async_computation.11 | async-start | bytes 10616832 | tf_op jit(solution)/shard_map/while/body/eval_jaxpr/reduce_scatter | solution.py:38
  1383.1 176.0 %reduce-scatter.7.cloned.1.call-start = ((), (), s32[]{:S(2)}) async-start(), calls=%async_computation.9 | async-start | bytes 10616832 | tf_op jit(solution)/shard_map/while/body/eval_jaxpr/reduce_scatter | solution.py:39
  1410.0 219.9 %reduce-scatter.5.cloned.1.call-start = ((), (), s32[]{:S(2)}) async-start(), calls=%async_computation.8 | async-start | bytes 10616832 | tf_op jit(solution)/shard_map/while/body/eval_jaxpr/reduce_scatter | solution.py:39
  1494.8 135.0 %copy-start = (f32[2,96,3072]{2,1,0:T(8,128)S(1)}, f32[2,96,3072]{2,1,0:T(8,128)}, u32[]{:S(2)}) copy-start(f32[2,96,3072]{2,1,0:T(8,128)} %get-tuple-element.230) | copy-start | bytes 7077892 | tf_op jit(solution)/shard_map/while
  1633.5 35.6 %all-gather.17.cloned.1.call-start = ((), (), s32[]{:S(2)}) async-start(), calls=%async_computation.4 | async-start | bytes 5308416 | tf_op jit(solution)/shard_map/while/body/eval_jaxpr/all_gather | solution.py:23
  1636.0 67.8 %all-gather.19.cloned.1.call-start = ((), (), s32[]{:S(2)}) async-start(), calls=%async_computation.5 | async-start | bytes 5308416 | tf_op jit(solution)/shard_map/while/body/eval_jaxpr/all_gather | solution.py:24
  1638.4 102.6 %all-gather.21.cloned.1.call-start = ((), (), s32[]{:S(2)}) async-start(), calls=%async_computation.6 | async-start | bytes 5308416 | tf_op jit(solution)/shard_map/while/body/eval_jaxpr/all_gather | solution.py:23
  1639.0 134.2 %all-gather.23.cloned.1.call-start = ((), (), s32[]{:S(2)}) async-start(), calls=%async_computation.7 | async-start | bytes 5308416 | tf_op jit(solution)/shard_map/while/body/eval_jaxpr/all_gather | solution.py:32
  1639.7 432.2 %reduce-scatter.9.cloned.1.call-start = ((), (), s32[]{:S(2)}) async-start(), calls=%async_computation.10 | async-start | bytes 10616832 | tf_op jit(solution)/shard_map/while/body/eval_jaxpr/reduce_scatter | solution.py:38
  1741.0 89.8 %slice-start = ((s8[4718592]{0:T(1024)(128)(4,1)}), s8[524288]{0:T(1024)(128)(4,1)S(1)}, s32[]{:S(2)}) async-start(s8[4718592]{0:T(1024)(128)(4,1)} %bitcast.128), calls=%async_computation.12 | async-start | bytes 1048576 | tf_op jit(solution)/shard_map/while
  1773.2 57.7 %slice-start.1 = ((s8[4718592]{0:T(1024)(128)(4,1)}), s8[4194304]{0:T(1024)(128)(4,1)S(1)}, s32[]{:S(2)}) async-start(s8[4718592]{0:T(1024)(128)(4,1)} %bitcast.128), calls=%async_computation.13 | async-start | bytes 8388608 | tf_op jit(solution)/shard_map/while
  1890.0 181.9 %reduce-scatter.11.cloned.1.call-start = ((), (), s32[]{:S(2)}) async-start(), calls=%async_computation.11 | async-start | bytes 10616832 | tf_op jit(solution)/shard_map/while/body/eval_jaxpr/reduce_scatter | solution.py:38
  1923.2 176.1 %reduce-scatter.7.cloned.1.call-start = ((), (), s32[]{:S(2)}) async-start(), calls=%async_computation.9 | async-start | bytes 10616832 | tf_op jit(solution)/shard_map/while/body/eval_jaxpr/reduce_scatter | solution.py:39
  1950.0 220.1 %reduce-scatter.5.cloned.1.call-start = ((), (), s32[]{:S(2)}) async-start(), calls=%async_computation.8 | async-start | bytes 10616832 | tf_op jit(solution)/shard_map/while/body/eval_jaxpr/reduce_scatter | solution.py:39
  2035.1 135.0 %copy-start = (f32[2,96,3072]{2,1,0:T(8,128)S(1)}, f32[2,96,3072]{2,1,0:T(8,128)}, u32[]{:S(2)}) copy-start(f32[2,96,3072]{2,1,0:T(8,128)} %get-tuple-element.230) | copy-start | bytes 7077892 | tf_op jit(solution)/shard_map/while
Sparse Core Ops, SparseCore 0:
  13.0 35.7 all-gather.16
  50.6 32.9 all-gather.18
  85.4 32.9 all-gather.20
  120.1 32.9 all-gather.22
  270.0 67.4 reduce-scatter.8
  340.7 67.4 reduce-scatter.10
  411.6 67.4 reduce-scatter.6
  482.5 67.4 reduce-scatter.4
  556.2 32.9 all-gather.16
  590.8 32.9 all-gather.18
  625.6 32.9 all-gather.20
  660.2 32.9 all-gather.22
  810.3 67.4 reduce-scatter.8
  881.0 67.4 reduce-scatter.10
  951.7 67.4 reduce-scatter.6
  1022.5 67.3 reduce-scatter.4
  1096.1 32.9 all-gather.16
  1130.8 32.9 all-gather.18
  1165.6 32.9 all-gather.20
  1200.2 32.9 all-gather.22
  1349.9 67.4 reduce-scatter.8
  1420.8 67.4 reduce-scatter.10
  1491.7 67.4 reduce-scatter.6
  1562.4 67.3 reduce-scatter.4
  1636.1 32.9 all-gather.16
  1670.8 32.9 all-gather.18
  1705.4 32.9 all-gather.20
  1740.2 32.9 all-gather.22
  1890.2 67.4 reduce-scatter.8
  1960.9 67.4 reduce-scatter.10
  2031.8 67.4 reduce-scatter.6
  2102.6 67.4 reduce-scatter.4
where the time goes:
time: 2180 us
  matrix products  1560 us (72%)
  waiting for transfers between devices  552 us (25%)
  other arithmetic  30.5 us (1%)
  local copies, waits for them, and re-layouts  22.2 us (1%)
    dot_general x8, matrix products, micro(): e = jnp.dot(gy, v2.T, preferred_element_type=jnp.float32)  461 us
    reduce_scatter x8, waiting for transfers between devices, micro(): lax.psum_scatter(p1, AX, scatter_dimension=0, tiled=True)  375 us
    dot_general x8, matrix products, micro(): jnp.dot(h, v2, preferred_element_type=jnp.float32)  296 us
    dot_general x8, matrix products, micro(): p2 = jnp.dot(h.T, gy, preferred_element_type=jnp.float32)  265 us
    dot_general x8, matrix products, micro(): p1 = jnp.dot(xl.T, da, preferred_element_type=jnp.float32)  217 us
    dot_general x8, matrix products, micro(): jnp.dot(cur, v1, preferred_element_type=jnp.float32).astype(jnp.bfloat16)  216 us
    all_gather x8, waiting for transfers between devices, micro(): v1 = lax.all_gather(w1[l], AX, axis=0, tiled=True)  120 us
    dot_general x4, matrix products, micro(): jnp.dot(da, v1.T, preferred_element_type=jnp.float32)  104 us
  transfers between devices with their start and end apart: 32, of which 20 were waited for; matrix products, arithmetic and copies ran while one was open for 51% of the time, Pallas kernels for 0%

commit v1 on v0

v1 whole, which is shorter than its diff:
```python
import functools
import math

import jax
import jax.numpy as jnp
from jax import lax
from jax.experimental import pallas as pl
from jax.experimental.pallas import tpu as pltpu
from jax.sharding import PartitionSpec as P

AX = "fsdp"
D, FF = 768, 3072
G0 = 768
HS = 1536
C0 = math.sqrt(2 / math.pi)
C1 = C0 * 0.044715
BF, F32 = jnp.bfloat16, jnp.float32


def gelu(a):
    t = jnp.tanh(a * (C0 + C1 * (a * a)))
    return a * (0.5 + 0.5 * t)


def gelu_grad(a):
    b = a * a
    s = 0.5 + 0.5 * jnp.tanh(a * (C0 + C1 * b))
    return s + ((a * s) * (1 - s)) * (2 * C0 + 6 * C1 * b)


def dot(a, b):
    return jnp.dot(a, b, preferred_element_type=F32)


def dot_nt(a, b):
    return lax.dot_general(a, b, (((1,), (1,)), ((), ())), preferred_element_type=F32)


def h_of(a):
    return gelu(a.astype(F32)).astype(BF)


def full(shape):
    return pl.BlockSpec(shape, lambda i: (0,) * len(shape), pipeline_mode=pl.Buffered(1))


def tok(bt, n):
    return pl.BlockSpec((bt, n), lambda i: (i, 0))


def sds(shape, dt=BF):
    return jax.ShapeDtypeStruct(shape, dt)


def call(name, body, t, bt, args, in_specs, out_specs, out_shape, scratch, dots):
    nbytes = sum(math.prod(v.shape) * v.dtype.itemsize for v in (*args, *out_shape))
    return pl.pallas_call(
        body, name=name, grid=(t // bt,), in_specs=in_specs, out_specs=out_specs, out_shape=out_shape,
        scratch_shapes=scratch,
        compiler_params=pltpu.CompilerParams(dimension_semantics=("arbitrary",), vmem_limit_bytes=67043328),
        cost_estimate=pl.CostEstimate(flops=int(dots * 2 * t * D * FF), bytes_accessed=nbytes, transcendentals=t * FF),
    )(*args)


def chunks(n, ch):
    return [slice(k, k + ch) for k in range(0, n, ch)]


def fwd_a(x, w, bt=1024, ch=256, h_from=None):
    t, n = x.shape[0], w.shape[1]

    def body(x_ref, w_ref, a_ref, *h_ref):
        lo = n if h_from is None else h_from
        prev = None
        for s in chunks(n, ch)[lo // ch:] + chunks(lo, ch):
            a = dot(x_ref[...], w_ref[:, s]).astype(BF)
            a_ref[:, s] = a
            if prev is not None:
                p, v = prev
                h_ref[0][:, p.start - lo:p.stop - lo] = h_of(v)
            prev = (s, a) if s.start >= lo else None

    widths = [n] if h_from is None else [n, n - h_from]
    return call(f"fwd_a{n}", body, t, bt, (x, w), [tok(bt, D), full((D, n))],
                [tok(bt, k) for k in widths], [sds((t, k)) for k in widths], [], n / FF)


def fwd_y0(x, a0, a1, h1, w2, bt=1024, ch=256):
    t = x.shape[0]

    def body(x_ref, a0_ref, a1_ref, h1_ref, w2_ref, y_ref, h_ref):
        for s in chunks(G0, ch):
            h_ref[:, s] = h_of(a0_ref[:, s])
        for s in chunks(HS - G0, ch):
            h_ref[:, G0 + s.start:G0 + s.stop] = h_of(a1_ref[:, s])
        p = dot(h1_ref[...], w2_ref[HS:, :]) + dot(h_ref[...], w2_ref[:HS, :])
        y_ref[...] = (x_ref[...].astype(F32) + p).astype(BF)

    return call("fwd_y0", body, t, bt, (x, a0, a1, h1, w2),
                [tok(bt, D), tok(bt, G0), tok(bt, HS - G0), tok(bt, FF - HS), full((FF, D))],
                [tok(bt, D)], [sds((t, D))], [pltpu.VMEM((bt, HS), BF)], 1)[0]


def fwd_y(x, h, w2, bt=1024):
    t = x.shape[0]

    def body(x_ref, h_ref, w2_ref, y_ref):
        y_ref[...] = (x_ref[...].astype(F32) + dot(h_ref[...], w2_ref[...])).astype(BF)

    return call("fwd_y", body, t, bt, (x, h, w2), [tok(bt, D), tok(bt, FF), full((FF, D))],
                [tok(bt, D)], [sds((t, D))], [], 1)[0]


def zero_first(ref):
    @pl.when(pl.program_id(0) == 0)
    def _():
        ref[...] = jnp.zeros_like(ref)


def put_last(steps, acc, out_ref, sem):
    @pl.when(pl.program_id(0) == steps - 1)
    def _():
        n, _, w = out_ref.shape
        copies = [pltpu.make_async_copy(acc.at[:, k * w:(k + 1) * w], out_ref.at[k], sem.at[k]) for k in range(n)]
        for c in copies:
            c.start()
        for c in copies:
            c.wait()


def fwd_dw2(x, g, w1, n, bt=512, ch=512):
    t = x.shape[0]

    def body(x_ref, g_ref, w1_ref, a_ref, h_ref, out_ref, acc, gT, sem):
        zero_first(acc)
        ss = chunks(FF, ch)

        def first(s):
            a = dot(x_ref[...], w1_ref[:, s]).astype(BF)
            a_ref[:, s] = a
            return a

        a, prev = first(ss[0]), None
        gT[...] = g_ref[...].T
        for j, s in enumerate(ss):
            nxt = first(ss[j + 1]) if j + 1 < len(ss) else None
            h = h_of(a)
            h_ref[:, s] = h
            if prev is not None:
                acc[:, ss[j - 1]] += dot(gT[...], prev)
            a, prev = nxt, h
        acc[:, ss[-1]] += dot(gT[...], prev)
        put_last(t // bt, acc, out_ref, sem)

    return call("fwd_dw2", body, t, bt, (x, g, w1), [tok(bt, D), tok(bt, D), full((D, FF))],
                [tok(bt, FF), tok(bt, FF), pl.BlockSpec(memory_space=pl.ANY)],
                [sds((t, FF)), sds((t, FF)), sds((n, D, FF // n), F32)],
                [pltpu.VMEM((D, FF), F32), pltpu.VMEM((D, bt), BF), pltpu.SemaphoreType.DMA((n,))], 2)


def dw2_0(g, a0, a1, h1, n, bt=1024, ch=512):
    t = g.shape[0]

    def body(g_ref, a0_ref, a1_ref, h1_ref, out_ref, acc, gT, h_ref, sem):
        zero_first(acc)
        gT[...] = g_ref[...].T
        for s in chunks(G0, 256):
            h_ref[:, s] = h_of(a0_ref[:, s])
        for s in chunks(HS - G0, 256):
            h_ref[:, G0 + s.start:G0 + s.stop] = h_of(a1_ref[:, s])
        for s in chunks(FF - HS, ch):
            acc[:, HS + s.start:HS + s.stop] += dot(gT[...], h1_ref[:, s])
        for s in chunks(HS, ch):
            acc[:, s] += dot(gT[...], h_ref[:, s])
        put_last(t // bt, acc, out_ref, sem)

    return call("dw2_0", body, t, bt, (g, a0, a1, h1),
                [tok(bt, D), tok(bt, G0), tok(bt, HS - G0), tok(bt, FF - HS)],
                [pl.BlockSpec(memory_space=pl.ANY)], [sds((n, D, FF // n), F32)],
                [pltpu.VMEM((D, FF), F32), pltpu.VMEM((D, bt), BF), pltpu.VMEM((bt, HS), BF),
                 pltpu.SemaphoreType.DMA((n,))], 1)[0]


def bwd(x, g, a, w2, w1=None, bt=512, ch=256, gq=1536):
    t = x.shape[0]
    na = len(a)

    def body(*refs):
        x_ref, g_ref, w2_ref, *rest = refs
        a_refs, rest = rest[:na], rest[na:]
        if w1 is None:
            dw_ref, xT = rest
        else:
            w1_ref, gx_ref, dw_ref, xT, gx_acc, da_ref = rest
        zero_first(dw_ref)
        work, off = [], 0
        for r in a_refs:
            for s in chunks(r.shape[1], ch):
                work.append((slice(off + s.start, off + s.stop), r, s))
            off += r.shape[1]

        def cot(k):
            return dot_nt(g_ref[...], w2_ref[work[k][0], :])

        def use(k, da):
            s = work[k][0]
            dw_ref[:, s] += dot(xT[...], da)
            if w1 is not None and s.stop % gq == 0:
                q = slice(s.stop - gq, s.stop)
                p = dot_nt(da_ref[:, q], w1_ref[:, q])
                if q.start:
                    p += gx_acc[...]
                if q.stop < FF:
                    gx_acc[...] = p
                else:
                    gx_ref[...] = (g_ref[...].astype(F32) + p).astype(BF)

        e, prev = cot(0), None
        xT[...] = x_ref[...].T
        for k, (_, r, s) in enumerate(work):
            nxt = cot(k + 1) if k + 1 < len(work) else None
            da = (gelu_grad(r[:, s].astype(F32)) * e).astype(BF)
            if w1 is not None:
                da_ref[:, work[k][0]] = da
            if prev is not None:
                use(k - 1, prev)
            e, prev = nxt, da
        use(len(work) - 1, prev)

    args, specs = [x, g, w2, *a], [tok(bt, D), tok(bt, D), full((FF, D)), *(tok(bt, v.shape[1]) for v in a)]
    outs, oshape = [full((D, FF))], [sds((D, FF), F32)]
    scratch = [pltpu.VMEM((D, bt), BF)]
    if w1 is not None:
        args, specs = [*args, w1], [*specs, full((D, FF))]
        outs, oshape = [tok(bt, D), *outs], [sds((t, D)), *oshape]
        scratch += [pltpu.VMEM((bt, D), F32), pltpu.VMEM((bt, FF), BF)]
    return call("bwd" if w1 is not None else "bwd0", body, t, bt, tuple(args), specs, outs, oshape, scratch,
                2 if w1 is None else 3)


def solution(mesh):
    spec = P(None, AX, None)
    n = mesh.shape[AX]

    def gather(w):
        return lax.all_gather(w, AX, axis=0, tiled=True)

    def scatter(v):
        return lax.psum_scatter(v, AX, scatter_dimension=0, tiled=True)

    def after(v, *done):
        return lax.optimization_barrier((v, *done))[0]

    def body(x, g, w1, w2):
        shape = x.shape
        x, g = x.reshape(-1, D), g.reshape(-1, D)
        w10a, w10b = gather(w1[0, :, :G0]), gather(w1[0, :, G0:])
        w20, w11, w21 = gather(w2[0]), gather(w1[1]), gather(w2[1])
        a0, = fwd_a(x, w10a)
        a1, h1 = fwd_a(after(x, a0), w10b, h_from=HS - G0)
        x1 = fwd_y0(x, a0, a1, h1, w20)
        a, h, p21 = fwd_dw2(x1, g, w11, n)
        s21 = scatter(p21)
        gx, p11 = bwd(x1, g, [a], w21, w11, bt=1024)
        s11 = scatter(p11)
        gx = after(gx, s21)
        p20 = dw2_0(gx, a0, a1, h1, n)
        s20 = scatter(p20)
        gx = after(gx, p20, s11)
        p10, = bwd(x, gx, [a0, a1], w20, bt=1024)
        s10 = scatter(p10)
        d2 = jnp.stack([s20.reshape(D, -1).T, s21.reshape(D, -1).T])
        y, s10 = lax.optimization_barrier((fwd_y(after(x1, p10), h, w21), s10))
        return y.reshape(shape), jnp.stack([s10, s11]), d2

    return jax.shard_map(body, mesh=mesh, in_specs=(spec, spec, spec, spec),
                         out_specs=(spec, spec, spec), check_vma=False)
```

time: 2180 us -> 1120 us (0.51)
  matrix products: 1560 us -> 0 us
  Pallas kernels: 0 us -> 1020 us
  waiting for transfers between devices: 552 us -> 69.6 us
  other arithmetic: 30.5 us -> 4.64 us
    dot_general x44 -> x0, matrix products: 1560 us -> none  [the longest x8 461 us: micro(): e = jnp.dot(gy, v2.T, preferred_element_type=jnp.float32)]
    pallas_call x0 -> x8, Pallas kernels: none -> 1020 us  [call(): pl.pallas_call(body, name=name, grid=(t // bt,), in_specs=in_specs, out_s...]
    reduce_scatter x16 -> x4, waiting for transfers between devices: 375 us -> 50.5 us  [scatter(): return lax.psum_scatter(v, AX, scatter_dimension=0, tiled=True)]
    all_gather x16 -> x5, waiting for transfers between devices: 172 us -> 17.7 us  [gather(): return lax.all_gather(w, AX, axis=0, tiled=True)]
    another operation x16 -> x2, other arithmetic: 30.5 us -> 4.64 us  [the longest x1 2.86 us: body(): return (y.reshape(shape), jnp.stack([s10, s11]), d2)]
  transfers between devices with their start and end apart: 32 -> 9, of which waited for: 20 -> 2; matrix products, arithmetic and copies ran while one was open for 51% -> 0% of each run, Pallas kernels for 0% -> 76%
where the time goes in v1:
time: 1120 us; the launch traced here: 1110 us
  Pallas kernels  1020 us (91%)
  waiting for transfers between devices  69.6 us (6%)
  between operations  14.2 us (1%)
    pallas_call x8, Pallas kernels, call(): pl.pallas_call(body, name=name, grid=(t // bt,), in_specs=in_specs, out_s...  1020 us
    reduce_scatter x4, waiting for transfers between devices, scatter(): return lax.psum_scatter(v, AX, scatter_dimension=0, tiled=True)  50.5 us
  transfers between devices with their start and end apart: 9, of which 2 were waited for; matrix products, arithmetic and copies ran while one was open for 0% of the time, Pallas kernels for 76%

profile of v1, /device:TPU:0, one launch (start us, length us, event | category | flops | bytes accessed | tf_op | source)
XLA Modules:
  0.0 1113.2 jit_solution(8379545479466045236)
XLA Ops:
  7.2 0.0 copy-start
  7.2 0.0 copy-start.1
  7.2 0.0 all-gather.11.cloned.1.call-start
  7.2 1.7 slice.15
  9.0 0.0 all-gather.11.cloned.1.call-update
  9.0 0.0 all-gather.13.cloned.1.call-start
  9.0 1.8 slice.16
  10.8 0.0 all-gather.13.cloned.1.call-update
  10.9 0.0 all-gather.15.cloned.1.call-start
  10.9 0.0 copy-done
  10.9 1.1 fusion
  12.0 0.0 all-gather.15.cloned.1.call-update
  12.0 0.0 all-gather.19.cloned.1.call-start
  12.1 0.0 copy-done.1
  12.1 0.9 slice.19
  13.0 0.0 all-gather.19.cloned.1.call-update
  13.0 0.0 all-gather.17.cloned.1.call-start
  13.0 0.5 all-gather.17.cloned.1.call-update
  13.6 0.0 reduce-scatter.5.cloned.1.call-start
  13.6 17.7 %all-gather.11.cloned.1.call-done = bf16[1,768,768]{2,1,0:T(8,128)(2,1)} async-done(((bf16[1,96,768]{2,1,0:T(8,128)(2,1)}), bf16[1,768,768]{2,1,0:T(8,128)(2,1)}) %all-gather.11.cloned.1.call-update) | async-done | bytes 1179664 | tf_op jit(solution)/shard_map/all_gather | solution.py:246
  31.3 30.0 %fwd_a768.1.a0_ref.refs_3_ = bf16[16384,768]{1,0:T(8,128)(2,1)} custom-call(bf16[16384,768]{1,0:T(8,128)(2,1)} %bitcast.26, bf16[768,768]{1,0:T(8,128)(2,1)} %bitcast.37), custom_call_target="tpu_custom_call" | custom-call | flops 19327352832 | bytes 51511296 | tf_op jit(solution)/shard_map/fwd_a768/pallas_call | solution.py:57
  61.4 0.0 all-gather.13.cloned.1.call-done
  61.4 80.4 %fwd_a2304.1 = (bf16[16384,2304]{1,0:T(8,128)(2,1)}, bf16[16384,1536]{1,0:T(8,128)(2,1)}) custom-call(bf16[16384,768]{1,0:T(8,128)(2,1)} %bitcast.27, bf16[768,2304]{1,0:T(8,128)(2,1)} %bitcast.36), custom_call_target="tpu_custom_call" | custom-call | flops 57982058496 | bytes 154533888 | tf_op jit(solution)/shard_map/fwd_a2304/pallas_call | solution.py:57
  141.8 0.0 all-gather.15.cloned.1.call-done
  141.8 93.1 %fwd_y0.1.x_ref.refs_0_ = bf16[16384,768]{1,0:T(8,128)(2,1)} custom-call(bf16[16384,768]{1,0:T(8,128)(2,1)} %bitcast.28, bf16[16384,768]{1,0:T(8,128)(2,1)} %fwd_a768.1.a0_ref.refs_3_, bf16[16384,2304]{1,0:T(8,128)(2,1)} %get-tuple-element.17.a1_ref.refs_4_, bf16[16384,1536]{1,0:T(8,128)(2,1)} %get-tuple-element.18.h1_ref, bf16[3072,768]{1,0:T(8,128)(2,1)} %bitcast.30), custom_call_target="tpu_custom_call" | custom-call | flops 77309411328 | bytes 206045184 | tf_op jit(solution)/shard_map/fwd_y0/pallas_call | solution.py:57
  234.9 0.0 all-gather.19.cloned.1.call-done
  234.9 193.4 %fwd_dw2.1 = (bf16[16384,3072]{1,0:T(8,128)(2,1)}, bf16[16384,3072]{1,0:T(8,128)(2,1)}, f32[8,768,384]{2,1,0:T(8,128)}) custom-call(bf16[16384,768]{1,0:T(8,128)(2,1)} %fwd_y0.1.x_ref.refs_0_, bf16[16384,768]{1,0:T(8,128)(2,1)} %bitcast.24, bf16[768,3072]{1,0:T(8,128)(2,1)} %bitcast.34), custom_call_target="tpu_custom_call" | custom-call | flops 154618822656 | bytes 265814016 | tf_op jit(solution)/shard_map/fwd_dw2/pallas_call | solution.py:57
  428.4 0.0 reduce-scatter.5.cloned.1.call-update
  428.4 0.0 reduce-scatter.7.cloned.1.call-start
  428.4 0.0 all-gather.17.cloned.1.call-done
  428.5 268.9 %bwd.1 = (bf16[16384,768]{1,0:T(8,128)(2,1)}, f32[768,3072]{1,0:T(8,128)}) custom-call(bf16[16384,768]{1,0:T(8,128)(2,1)} %fwd_y0.1.x_ref.refs_0_, bf16[16384,768]{1,0:T(8,128)(2,1)} %bitcast.25, bf16[3072,768]{1,0:T(8,128)(2,1)} %bitcast.32, bf16[16384,3072]{1,0:T(8,128)(2,1)} %get-tuple-element.19.refs_3_, bf16[768,3072]{1,0:T(8,128)(2,1)} %bitcast.35), custom_call_target="tpu_custom_call" | custom-call | flops 231928233984 | bytes 195035136 | tf_op jit(solution)/shard_map/bwd/pallas_call | solution.py:57
  697.4 0.0 reduce-scatter.7.cloned.1.call-update
  697.4 0.0 reduce-scatter.9.cloned.1.call-start
  697.5 0.0 reduce-scatter.5.cloned.1.call-done
  697.5 89.6 %dw2_0.1 = f32[8,768,384]{2,1,0:T(8,128)} custom-call(bf16[16384,768]{1,0:T(8,128)(2,1)} %get-tuple-element.24.g_ref.refs_1_, bf16[16384,768]{1,0:T(8,128)(2,1)} %fwd_a768.1.a0_ref.refs_3_, bf16[16384,2304]{1,0:T(8,128)(2,1)} %get-tuple-element.17.a1_ref.refs_4_, bf16[16384,1536]{1,0:T(8,128)(2,1)} %get-tuple-element.18.h1_ref), custom_call_target="tpu_custom_call" | custom-call | flops 77309411328 | bytes 185597952 | tf_op jit(solution)/shard_map/dw2_0/pallas_call | solution.py:57
  787.1 0.0 reduce-scatter.7.cloned.1.call-done
  787.2 174.2 %bwd0.1 = f32[768,3072]{1,0:T(8,128)} custom-call(bf16[16384,768]{1,0:T(8,128)(2,1)} %bitcast.29, bf16[16384,768]{1,0:T(8,128)(2,1)} %get-tuple-element.24.g_ref.refs_1_, bf16[3072,768]{1,0:T(8,128)(2,1)} %bitcast.31, bf16[16384,768]{1,0:T(8,128)(2,1)} %fwd_a768.1.a0_ref.refs_3_, bf16[16384,2304]{1,0:T(8,128)(2,1)} %get-tuple-element.17.a1_ref.refs_4_), custom_call_target="tpu_custom_call" | custom-call | flops 154618822656 | bytes 165150720 | tf_op jit(solution)/shard_map/bwd0/pallas_call | solution.py:57
  961.3 0.0 reduce-scatter.9.cloned.1.call-update
  961.4 0.0 reduce-scatter.11.cloned.1.call-start
  961.4 0.7 reduce-scatter.11.cloned.1.call-update
  962.1 87.3 %fwd_y.1 = bf16[16384,768]{1,0:T(8,128)(2,1)} custom-call(bf16[16384,768]{1,0:T(8,128)(2,1)} %fwd_y0.1.x_ref.refs_0_, bf16[16384,3072]{1,0:T(8,128)(2,1)} %get-tuple-element.26.h_ref, bf16[3072,768]{1,0:T(8,128)(2,1)} %bitcast.33), custom_call_target="tpu_custom_call" | custom-call | flops 77309411328 | bytes 155713536 | tf_op jit(solution)/shard_map/fwd_y/pallas_call | solution.py:57
  1049.4 0.0 reduce-scatter.9.cloned.1.call-done
  1049.4 50.5 %reduce-scatter.11.cloned.1.call-done = f32[1,768,384]{2,1,0:T(8,128)} async-done(((f32[8,768,384]{2,1,0:T(8,128)}), f32[1,768,384]{2,1,0:T(8,128)}) %reduce-scatter.11.cloned.1.call-update) | async-done | bytes 1179664 | tf_op jit(solution)/shard_map/reduce_scatter | solution.py:249
  1099.8 1.8 pad_maximum_fusion.1
  1101.6 0.0 copy-start.2
  1101.6 2.0 copy.7
  1103.6 0.0 copy-done.2
  1103.6 2.9 pad_maximum_fusion
Async XLA Ops:
  7.2 3.8 copy-start
  7.2 4.9 copy-start.1
  7.2 24.2 %all-gather.11.cloned.1.call-start = ((), (), s32[]{:S(2)}) async-start(), calls=%async_computation.8 | async-start | bytes 1327104 | tf_op jit(solution)/shard_map/all_gather | solution.py:246
  9.0 52.4 %all-gather.13.cloned.1.call-start = ((), (), s32[]{:S(2)}) async-start(), calls=%async_computation.9 | async-start | bytes 3981312 | tf_op jit(solution)/shard_map/all_gather | solution.py:246
  10.9 130.9 %all-gather.15.cloned.1.call-start = ((), (), s32[]{:S(2)}) async-start(), calls=%async_computation.10 | async-start | bytes 5308416 | tf_op jit(solution)/shard_map/all_gather | solution.py:246
  12.0 222.9 %all-gather.19.cloned.1.call-start = ((), (), s32[]{:S(2)}) async-start(), calls=%async_computation.12 | async-start | bytes 5308416 | tf_op jit(solution)/shard_map/all_gather | solution.py:246
  13.0 415.5 %all-gather.17.cloned.1.call-start = ((), (), s32[]{:S(2)}) async-start(), calls=%async_computation.11 | async-start | bytes 5308416 | tf_op jit(solution)/shard_map/all_gather | solution.py:246
  13.6 683.9 %reduce-scatter.5.cloned.1.call-start = ((), (), s32[]{:S(2)}) async-start(), calls=%async_computation.4 | async-start | bytes 10616832 | tf_op jit(solution)/shard_map/reduce_scatter | solution.py:249
  428.4 358.8 %reduce-scatter.7.cloned.1.call-start = ((), (), s32[]{:S(2)}) async-start(), calls=%async_computation.5 | async-start | bytes 10616832 | tf_op jit(solution)/shard_map/reduce_scatter | solution.py:249
  697.4 351.9 %reduce-scatter.9.cloned.1.call-start = ((), (), s32[]{:S(2)}) async-start(), calls=%async_computation.6 | async-start | bytes 10616832 | tf_op jit(solution)/shard_map/reduce_scatter | solution.py:249
  961.4 138.5 %reduce-scatter.11.cloned.1.call-start = ((), (), s32[]{:S(2)}) async-start(), calls=%async_computation.7 | async-start | bytes 10616832 | tf_op jit(solution)/shard_map/reduce_scatter | solution.py:249
  1101.6 2.0 copy-start.2
Sparse Core Ops, SparseCore 0:
  10.4 20.9 all-gather.10
  33.1 27.9 all-gather.12
  63.6 32.9 all-gather.14
  98.2 32.9 all-gather.18
  133.5 32.9 all-gather.16
  428.5 67.4 reduce-scatter.4
  697.5 67.4 reduce-scatter.6
  961.5 67.4 reduce-scatter.8
  1032.4 67.3 reduce-scatter.10

commit v2 on v1

--- a/solution.py
+++ b/solution.py
@@ -11,7 +11,6 @@
 AX = "fsdp"
 D, FF = 768, 3072
 G0 = 768
-HS = 1536
 C0 = math.sqrt(2 / math.pi)
 C1 = C0 * 0.044715
 BF, F32 = jnp.bfloat16, jnp.float32
@@ -66,49 +65,43 @@
     return [slice(k, k + ch) for k in range(0, n, ch)]
 
 
-def fwd_a(x, w, bt=1024, ch=256, h_from=None):
+def pieces(refs, ch):
+    work, off = [], 0
+    for r in refs:
+        work += [(slice(off + s.start, off + s.stop), r, s) for s in chunks(r.shape[1], ch)]
+        off += r.shape[1]
+    return work
+
+
+def fwd_a(x, w, bt=1024, ch=256):
     t, n = x.shape[0], w.shape[1]
 
-    def body(x_ref, w_ref, a_ref, *h_ref):
-        lo = n if h_from is None else h_from
-        prev = None
-        for s in chunks(n, ch)[lo // ch:] + chunks(lo, ch):
-            a = dot(x_ref[...], w_ref[:, s]).astype(BF)
-            a_ref[:, s] = a
-            if prev is not None:
-                p, v = prev
-                h_ref[0][:, p.start - lo:p.stop - lo] = h_of(v)
-            prev = (s, a) if s.start >= lo else None
-
-    widths = [n] if h_from is None else [n, n - h_from]
-    return call(f"fwd_a{n}", body, t, bt, (x, w), [tok(bt, D), full((D, n))],
-                [tok(bt, k) for k in widths], [sds((t, k)) for k in widths], [], n / FF)
-
-
-def fwd_y0(x, a0, a1, h1, w2, bt=1024, ch=256):
-    t = x.shape[0]
-
-    def body(x_ref, a0_ref, a1_ref, h1_ref, w2_ref, y_ref, h_ref):
-        for s in chunks(G0, ch):
-            h_ref[:, s] = h_of(a0_ref[:, s])
-        for s in chunks(HS - G0, ch):
-            h_ref[:, G0 + s.start:G0 + s.stop] = h_of(a1_ref[:, s])
-        p = dot(h1_ref[...], w2_ref[HS:, :]) + dot(h_ref[...], w2_ref[:HS, :])
-        y_ref[...] = (x_ref[...].astype(F32) + p).astype(BF)
-
-    return call("fwd_y0", body, t, bt, (x, a0, a1, h1, w2),
-                [tok(bt, D), tok(bt, G0), tok(bt, HS - G0), tok(bt, FF - HS), full((FF, D))],
-                [tok(bt, D)], [sds((t, D))], [pltpu.VMEM((bt, HS), BF)], 1)[0]
-
-
-def fwd_y(x, h, w2, bt=1024):
-    t = x.shape[0]
-
-    def body(x_ref, h_ref, w2_ref, y_ref):
-        y_ref[...] = (x_ref[...].astype(F32) + dot(h_ref[...], w2_ref[...])).astype(BF)
-
-    return call("fwd_y", body, t, bt, (x, h, w2), [tok(bt, D), tok(bt, FF), full((FF, D))],
-                [tok(bt, D)], [sds((t, D))], [], 1)[0]
+    def body(x_ref, w_ref, a_ref):
+        for s in chunks(n, ch):
+            a_ref[:, s] = dot(x_ref[...], w_ref[:, s]).astype(BF)
+
+    return call(f"fwd_a{n}", body, t, bt, (x, w), [tok(bt, D), full((D, n))], [tok(bt, n)], [sds((t, n))], [], n / FF)[0]
+
+
+def fwd_y(x, a, w2, name, bt=1024, ch=256, rs=128):
+    t, na = x.shape[0], len(a)
+
+    def body(x_ref, w2_ref, *refs):
+        y_ref, h_ref = refs[na:]
+
+        def act(r):
+            for c, ref, s in pieces(refs[:na], ch):
+                h_ref[r, c] = h_of(ref[r, s])
+
+        rows = chunks(bt, rs)
+        act(rows[0])
+        for k, r in enumerate(rows):
+            if k + 1 < len(rows):
+                act(rows[k + 1])
+            y_ref[r, :] = (x_ref[r, :].astype(F32) + dot(h_ref[r, :], w2_ref[...])).astype(BF)
+
+    return call(name, body, t, bt, (x, w2, *a), [tok(bt, D), full((FF, D)), *(tok(bt, v.shape[1]) for v in a)],
+                [tok(bt, D)], [sds((t, D))], [pltpu.VMEM((bt, FF), BF)], 1)[0]
 
 
 def zero_first(ref):
@@ -128,10 +121,10 @@
             c.wait()
 
 
-def fwd_dw2(x, g, w1, n, bt=512, ch=512):
+def fwd_dw2(x, g, w1, n, bt=1024, ch=256):
     t = x.shape[0]
 
-    def body(x_ref, g_ref, w1_ref, a_ref, h_ref, out_ref, acc, gT, sem):
+    def body(x_ref, g_ref, w1_ref, a_ref, out_ref, acc, gT, sem):
         zero_first(acc)
         ss = chunks(FF, ch)
 
@@ -145,7 +138,6 @@
         for j, s in enumerate(ss):
             nxt = first(ss[j + 1]) if j + 1 < len(ss) else None
             h = h_of(a)
-            h_ref[:, s] = h
             if prev is not None:
                 acc[:, ss[j - 1]] += dot(gT[...], prev)
             a, prev = nxt, h
@@ -153,35 +145,28 @@
         put_last(t // bt, acc, out_ref, sem)
 
     return call("fwd_dw2", body, t, bt, (x, g, w1), [tok(bt, D), tok(bt, D), full((D, FF))],
-                [tok(bt, FF), tok(bt, FF), pl.BlockSpec(memory_space=pl.ANY)],
-                [sds((t, FF)), sds((t, FF)), sds((n, D, FF // n), F32)],
+                [tok(bt, FF), pl.BlockSpec(memory_space=pl.ANY)],
+                [sds((t, FF)), sds((n, D, FF // n), F32)],
                 [pltpu.VMEM((D, FF), F32), pltpu.VMEM((D, bt), BF), pltpu.SemaphoreType.DMA((n,))], 2)
 
 
-def dw2_0(g, a0, a1, h1, n, bt=1024, ch=512):
-    t = g.shape[0]
-
-    def body(g_ref, a0_ref, a1_ref, h1_ref, out_ref, acc, gT, h_ref, sem):
+def dw2_0(g, a, n, bt=1024, ch=768):
+    t, na = g.shape[0], len(a)
+
+    def body(g_ref, *refs):
+        out_ref, acc, gT, sem = refs[na:]
         zero_first(acc)
         gT[...] = g_ref[...].T
-        for s in chunks(G0, 256):
-            h_ref[:, s] = h_of(a0_ref[:, s])
-        for s in chunks(HS - G0, 256):
-            h_ref[:, G0 + s.start:G0 + s.stop] = h_of(a1_ref[:, s])
-        for s in chunks(FF - HS, ch):
-            acc[:, HS + s.start:HS + s.stop] += dot(gT[...], h1_ref[:, s])
-        for s in chunks(HS, ch):
-            acc[:, s] += dot(gT[...], h_ref[:, s])
+        for c, r, s in pieces(refs[:na], ch):
+            acc[:, c] += dot(gT[...], h_of(r[:, s]))
         put_last(t // bt, acc, out_ref, sem)
 
-    return call("dw2_0", body, t, bt, (g, a0, a1, h1),
-                [tok(bt, D), tok(bt, G0), tok(bt, HS - G0), tok(bt, FF - HS)],
+    return call("dw2_0", body, t, bt, (g, *a), [tok(bt, D), *(tok(bt, v.shape[1]) for v in a)],
                 [pl.BlockSpec(memory_space=pl.ANY)], [sds((n, D, FF // n), F32)],
-                [pltpu.VMEM((D, FF), F32), pltpu.VMEM((D, bt), BF), pltpu.VMEM((bt, HS), BF),
-                 pltpu.SemaphoreType.DMA((n,))], 1)[0]
-
-
-def bwd(x, g, a, w2, w1=None, bt=512, ch=256, gq=1536):
+                [pltpu.VMEM((D, FF), F32), pltpu.VMEM((D, bt), BF), pltpu.SemaphoreType.DMA((n,))], 1)[0]
+
+
+def bwd(x, g, a, w2, w1=None, bt=512, ch=512, gq=1536):
     t = x.shape[0]
     na = len(a)
 
@@ -193,11 +178,7 @@
         else:
             w1_ref, gx_ref, dw_ref, xT, gx_acc, da_ref = rest
         zero_first(dw_ref)
-        work, off = [], 0
-        for r in a_refs:
-            for s in chunks(r.shape[1], ch):
-                work.append((slice(off + s.start, off + s.stop), r, s))
-            off += r.shape[1]
+        work = pieces(a_refs, ch)
 
         def cot(k):
             return dot_nt(g_ref[...], w2_ref[work[k][0], :])
@@ -256,21 +237,21 @@
         x, g = x.reshape(-1, D), g.reshape(-1, D)
         w10a, w10b = gather(w1[0, :, :G0]), gather(w1[0, :, G0:])
         w20, w11, w21 = gather(w2[0]), gather(w1[1]), gather(w2[1])
-        a0, = fwd_a(x, w10a)
-        a1, h1 = fwd_a(after(x, a0), w10b, h_from=HS - G0)
-        x1 = fwd_y0(x, a0, a1, h1, w20)
-        a, h, p21 = fwd_dw2(x1, g, w11, n)
+        a0 = [fwd_a(x, w10a)]
+        a0.append(fwd_a(after(x, a0[0]), w10b))
+        x1 = fwd_y(x, a0, w20, "fwd_y0")
+        a, p21 = fwd_dw2(x1, g, w11, n)
         s21 = scatter(p21)
         gx, p11 = bwd(x1, g, [a], w21, w11, bt=1024)
         s11 = scatter(p11)
         gx = after(gx, s21)
-        p20 = dw2_0(gx, a0, a1, h1, n)
+        p20 = dw2_0(gx, a0, n)
         s20 = scatter(p20)
         gx = after(gx, p20, s11)
-        p10, = bwd(x, gx, [a0, a1], w20, bt=1024)
+        p10, = bwd(x, gx, a0, w20, bt=1024, ch=256)
         s10 = scatter(p10)
+        y, s10 = lax.optimization_barrier((fwd_y(after(x1, p10, s20), [a], w21, "fwd_y1"), s10))
         d2 = jnp.stack([s20.reshape(D, -1).T, s21.reshape(D, -1).T])
-        y, s10 = lax.optimization_barrier((fwd_y(after(x1, p10), h, w21), s10))
         return y.reshape(shape), jnp.stack([s10, s11]), d2
 
     return jax.shard_map(body, mesh=mesh, in_specs=(spec, spec, spec, spec),

time: 1120 us -> 1040 us (0.929)
  waiting for transfers between devices: 69.6 us -> 18.4 us
  Pallas kernels: 1020 us -> 991 us
    reduce_scatter x4, waiting for transfers between devices: 50.5 us -> 0.06 us  [scatter(): return lax.psum_scatter(v, AX, scatter_dimension=0, tiled=True)]
    pallas_call x8, Pallas kernels: 1020 us -> 991 us  [call(): pl.pallas_call(body, name=name, grid=(t // bt,), in_specs=in_specs, out_s...]
  transfers between devices with their start and end apart: 9 -> 9, of which waited for: 2 -> 1; matrix products, arithmetic and copies ran while one was open for 0% -> 0% of each run, Pallas kernels for 76% -> 96%
where the time goes in v2:
time: 1040 us
  Pallas kernels  991 us (95%)
  waiting for transfers between devices  18.4 us (2%)
  between operations  14.2 us (1%)
    pallas_call x8, Pallas kernels, call(): pl.pallas_call(body, name=name, grid=(t // bt,), in_specs=in_specs, out_s...  991 us
  transfers between devices with their start and end apart: 9, of which 1 were waited for; matrix products, arithmetic and copies ran while one was open for 0% of the time, Pallas kernels for 96%

profile of v2, /device:TPU:0, one launch (start us, length us, event | category | flops | bytes accessed | tf_op | source)
XLA Modules:
  0.0 1036.1 jit_solution(269892253979384317)
XLA Ops:
  7.2 0.0 copy-start
  7.2 0.0 copy-start.1
  7.2 0.0 all-gather.13.cloned.1.call-start
  7.2 1.7 slice.16
  9.0 0.0 all-gather.13.cloned.1.call-update
  9.0 0.0 all-gather.15.cloned.1.call-start
  9.0 1.8 slice.17
  10.8 0.0 all-gather.15.cloned.1.call-update
  10.9 0.0 all-gather.11.cloned.1.call-start
  10.9 0.0 copy-done
  10.9 1.1 fusion
  12.0 0.0 all-gather.11.cloned.1.call-update
  12.0 0.0 all-gather.19.cloned.1.call-start
  12.1 0.0 copy-done.1
  12.1 0.9 slice.19
  13.0 0.0 all-gather.19.cloned.1.call-update
  13.0 0.0 all-gather.17.cloned.1.call-start
  13.1 0.5 all-gather.17.cloned.1.call-update
  13.6 0.0 reduce-scatter.5.cloned.1.call-start
  13.7 17.7 %all-gather.13.cloned.1.call-done = bf16[1,768,768]{2,1,0:T(8,128)(2,1)} async-done(((bf16[1,96,768]{2,1,0:T(8,128)(2,1)}), bf16[1,768,768]{2,1,0:T(8,128)(2,1)}) %all-gather.13.cloned.1.call-update) | async-done | bytes 1179664 | tf_op jit(solution)/shard_map/all_gather | solution.py:227
  31.3 30.0 %fwd_a768.1.refs_0_.refs_3_ = bf16[16384,768]{1,0:T(8,128)(2,1)} custom-call(bf16[16384,768]{1,0:T(8,128)(2,1)} %bitcast.26, bf16[768,768]{1,0:T(8,128)(2,1)} %bitcast.37), custom_call_target="tpu_custom_call" | custom-call | flops 19327352832 | bytes 51511296 | tf_op jit(solution)/shard_map/fwd_a768/pallas_call | solution.py:56
  61.4 0.0 all-gather.15.cloned.1.call-done
  61.4 66.2 %fwd_a2304.1.refs_1_.refs_4_ = bf16[16384,2304]{1,0:T(8,128)(2,1)} custom-call(bf16[16384,768]{1,0:T(8,128)(2,1)} %bitcast.27, bf16[768,2304]{1,0:T(8,128)(2,1)} %bitcast.36), custom_call_target="tpu_custom_call" | custom-call | flops 57982058496 | bytes 104202240 | tf_op jit(solution)/shard_map/fwd_a2304/pallas_call | solution.py:56
  127.6 0.0 all-gather.11.cloned.1.call-done
  127.6 97.4 %fwd_y0.1.x_ref.refs_0_ = bf16[16384,768]{1,0:T(8,128)(2,1)} custom-call(bf16[16384,768]{1,0:T(8,128)(2,1)} %bitcast.28, bf16[3072,768]{1,0:T(8,128)(2,1)} %bitcast.30, bf16[16384,768]{1,0:T(8,128)(2,1)} %fwd_a768.1.refs_0_.refs_3_, bf16[16384,2304]{1,0:T(8,128)(2,1)} %fwd_a2304.1.refs_1_.refs_4_), custom_call_target="tpu_custom_call" | custom-call | flops 77309411328 | bytes 155713536 | tf_op jit(solution)/shard_map/fwd_y0/pallas_call | solution.py:56
  225.0 0.0 all-gather.19.cloned.1.call-done
  225.0 170.6 %fwd_dw2.1 = (bf16[16384,3072]{1,0:T(8,128)(2,1)}, f32[8,768,384]{2,1,0:T(8,128)}) custom-call(bf16[16384,768]{1,0:T(8,128)(2,1)} %fwd_y0.1.x_ref.refs_0_, bf16[16384,768]{1,0:T(8,128)(2,1)} %bitcast.24, bf16[768,3072]{1,0:T(8,128)(2,1)} %bitcast.34), custom_call_target="tpu_custom_call" | custom-call | flops 154618822656 | bytes 165150720 | tf_op jit(solution)/shard_map/fwd_dw2/pallas_call | solution.py:56
  395.6 0.0 reduce-scatter.5.cloned.1.call-update
  395.6 0.0 reduce-scatter.7.cloned.1.call-start
  395.7 0.0 all-gather.17.cloned.1.call-done
  395.7 264.1 %bwd.1 = (bf16[16384,768]{1,0:T(8,128)(2,1)}, f32[768,3072]{1,0:T(8,128)}) custom-call(bf16[16384,768]{1,0:T(8,128)(2,1)} %fwd_y0.1.x_ref.refs_0_, bf16[16384,768]{1,0:T(8,128)(2,1)} %bitcast.25, bf16[3072,768]{1,0:T(8,128)(2,1)} %bitcast.32, bf16[16384,3072]{1,0:T(8,128)(2,1)} %get-tuple-element.14.refs_3_.refs_0_, bf16[768,3072]{1,0:T(8,128)(2,1)} %bitcast.35), custom_call_target="tpu_custom_call" | custom-call | flops 231928233984 | bytes 195035136 | tf_op jit(solution)/shard_map/bwd/pallas_call | solution.py:56
  659.8 0.0 reduce-scatter.7.cloned.1.call-update
  659.8 0.0 reduce-scatter.9.cloned.1.call-start
  659.8 0.0 reduce-scatter.5.cloned.1.call-done
  659.9 91.3 %dw2_0.1 = f32[8,768,384]{2,1,0:T(8,128)} custom-call(bf16[16384,768]{1,0:T(8,128)(2,1)} %get-tuple-element.19.g_ref.refs_1_, bf16[16384,768]{1,0:T(8,128)(2,1)} %fwd_a768.1.refs_0_.refs_3_, bf16[16384,2304]{1,0:T(8,128)(2,1)} %fwd_a2304.1.refs_1_.refs_4_), custom_call_target="tpu_custom_call" | custom-call | flops 77309411328 | bytes 135266304 | tf_op jit(solution)/shard_map/dw2_0/pallas_call | solution.py:56
  751.2 0.0 reduce-scatter.9.cloned.1.call-update
  751.2 0.0 reduce-scatter.11.cloned.1.call-start
  751.3 0.0 reduce-scatter.7.cloned.1.call-done
  751.3 174.2 %bwd0.1 = f32[768,3072]{1,0:T(8,128)} custom-call(bf16[16384,768]{1,0:T(8,128)(2,1)} %bitcast.29, bf16[16384,768]{1,0:T(8,128)(2,1)} %get-tuple-element.19.g_ref.refs_1_, bf16[3072,768]{1,0:T(8,128)(2,1)} %bitcast.31, bf16[16384,768]{1,0:T(8,128)(2,1)} %fwd_a768.1.refs_0_.refs_3_, bf16[16384,2304]{1,0:T(8,128)(2,1)} %fwd_a2304.1.refs_1_.refs_4_), custom_call_target="tpu_custom_call" | custom-call | flops 154618822656 | bytes 165150720 | tf_op jit(solution)/shard_map/bwd0/pallas_call | solution.py:56
  925.5 0.0 reduce-scatter.11.cloned.1.call-update
  925.5 0.0 reduce-scatter.9.cloned.1.call-done
  925.6 97.2 %fwd_y1.1 = bf16[16384,768]{1,0:T(8,128)(2,1)} custom-call(bf16[16384,768]{1,0:T(8,128)(2,1)} %fwd_y0.1.x_ref.refs_0_, bf16[3072,768]{1,0:T(8,128)(2,1)} %bitcast.33, bf16[16384,3072]{1,0:T(8,128)(2,1)} %get-tuple-element.14.refs_3_.refs_0_), custom_call_target="tpu_custom_call" | custom-call | flops 77309411328 | bytes 155713536 | tf_op jit(solution)/shard_map/fwd_y1/pallas_call | solution.py:56
  1022.7 0.0 reduce-scatter.11.cloned.1.call-done
  1022.7 1.8 pad_maximum_fusion.1
  1024.5 0.0 copy-start.2
  1024.5 2.0 copy.7
  1026.5 0.0 copy-done.2
  1026.5 2.9 pad_maximum_fusion
Async XLA Ops:
  7.2 3.8 copy-start
  7.2 4.9 copy-start.1
  7.2 24.2 %all-gather.13.cloned.1.call-start = ((), (), s32[]{:S(2)}) async-start(), calls=%async_computation.9 | async-start | bytes 1327104 | tf_op jit(solution)/shard_map/all_gather | solution.py:227
  9.0 52.4 %all-gather.15.cloned.1.call-start = ((), (), s32[]{:S(2)}) async-start(), calls=%async_computation.10 | async-start | bytes 3981312 | tf_op jit(solution)/shard_map/all_gather | solution.py:227
  10.9 116.7 %all-gather.11.cloned.1.call-start = ((), (), s32[]{:S(2)}) async-start(), calls=%async_computation.8 | async-start | bytes 5308416 | tf_op jit(solution)/shard_map/all_gather | solution.py:227
  12.0 213.0 %all-gather.19.cloned.1.call-start = ((), (), s32[]{:S(2)}) async-start(), calls=%async_computation.12 | async-start | bytes 5308416 | tf_op jit(solution)/shard_map/all_gather | solution.py:227
  13.0 382.7 %all-gather.17.cloned.1.call-start = ((), (), s32[]{:S(2)}) async-start(), calls=%async_computation.11 | async-start | bytes 5308416 | tf_op jit(solution)/shard_map/all_gather | solution.py:227
  13.6 646.2 %reduce-scatter.5.cloned.1.call-start = ((), (), s32[]{:S(2)}) async-start(), calls=%async_computation.4 | async-start | bytes 10616832 | tf_op jit(solution)/shard_map/reduce_scatter | solution.py:230
  395.6 355.7 %reduce-scatter.7.cloned.1.call-start = ((), (), s32[]{:S(2)}) async-start(), calls=%async_computation.5 | async-start | bytes 10616832 | tf_op jit(solution)/shard_map/reduce_scatter | solution.py:230
  659.8 265.8 %reduce-scatter.9.cloned.1.call-start = ((), (), s32[]{:S(2)}) async-start(), calls=%async_computation.6 | async-start | bytes 10616832 | tf_op jit(solution)/shard_map/reduce_scatter | solution.py:230
  751.2 271.5 %reduce-scatter.11.cloned.1.call-start = ((), (), s32[]{:S(2)}) async-start(), calls=%async_computation.7 | async-start | bytes 10616832 | tf_op jit(solution)/shard_map/reduce_scatter | solution.py:230
  1024.5 2.0 copy-start.2
Sparse Core Ops, SparseCore 0:
  10.4 20.9 all-gather.12
  33.1 27.9 all-gather.14
  63.6 32.9 all-gather.10
  98.2 32.9 all-gather.18
  133.4 32.9 all-gather.16
  395.7 67.4 reduce-scatter.4
  659.9 67.4 reduce-scatter.6
  751.3 67.4 reduce-scatter.8
  925.7 67.4 reduce-scatter.10
